TPU v7x, 32 devices: a whole 2x2x4 slice. The times are simulated.
32 devices in a mesh: section: 4 (over x, core), expert: 8 (over z, y).
Axes of the slice: x: 2, y: 2, z: 4, core: 2. Of those that a mesh axis runs over, the one named last changes fastest.
Arguments:
- x_fwd: bfloat16 [4, 1024, 3584], P('section', 'expert'), may hold values from -6 to 6
- routes_fwd: int32 [4, 1024, 2], P('section', 'expert'), may hold values from 0 to 3, all different within a row; in each aligned block of 128 rows (0 to 127, 128 to 255, ..., all dimensions but the last counted through in order) at most 96 rows name the same one
- affinity_fwd: float32 [4, 1024, 2], P('section', 'expert'), may hold values from 0.1 to 1
- x_bwd: bfloat16 [4, 1024, 3584], P('section', 'expert'), may hold values from -6 to 6
- grad_bwd: bfloat16 [4, 1024, 3584], P('section', 'expert'), may hold values from -6 to 6
- routes_bwd: int32 [4, 1024, 2], P('section', 'expert'), may hold values from 0 to 3, all different within a row; in each aligned block of 128 rows (0 to 127, 128 to 255, ..., all dimensions but the last counted through in order) at most 96 rows name the same one
- affinity_bwd: float32 [4, 1024, 2], P('section', 'expert'), may hold values from 0.1 to 1
- up_weight: bfloat16 [4, 3584, 4096], P('section', None, 'expert'), may hold values from -0.09375 to 0.09375
- down_weight: bfloat16 [4, 4096, 3584], P('section', 'expert'), may hold values from -0.1875 to 0.1875
Outputs:
- fwd_next: bfloat16 [4, 1024, 3584], P('section', 'expert')
- bwd_next: bfloat16 [4, 1024, 3584], P('section', 'expert')
Inputs may be any that keep to these rules, and one draw needn't show every extreme that they name: `routes_fwd`: each row names 2 different experts; in each section, among the 128 rows of one device (aligned blocks), no expert is named more than 96 times, a bound that some block reaches. `routes_bwd`: each row names 2 different experts; in each section, among the 128 rows of one device (aligned blocks), no expert is named more than 96 times, a bound that some block reaches.
All inputs are finite; a program needn't handle non-finite values.
Results may differ from a plain program's by a relative error of at most 0.0041.
Values may be sent and summed in bfloat16 or wider, within the bound.
A program may use at most 128 MiB of HBM per device.

v0:
```python
import functools

import jax
import jax.numpy as jnp
from jax import lax
from jax.experimental import pallas as pl
from jax.experimental.pallas import tpu as pltpu
from jax.sharding import PartitionSpec as P

AGAINST_ROWS = (((1,), (1,)), ((), ()))


def from_partner_2(block, axis, apart):
    count = lax.axis_size(axis)
    route = []
    for low in range(count):
        high = low | 1 << apart
        if high != low and high < count:
            route += [(low, high), (high, low)]
    return lax.ppermute(block, axis, route)


def shifted(shard, axis, by):
    size = lax.axis_size(axis)
    return lax.ppermute(shard, axis, [(i, (i + by) % size) for i in range(size)])


def silu_grad(values):
    sigma = jax.nn.sigmoid(values)
    return sigma * (1.0 + values * (1.0 - sigma))


def slot_table(routes, experts, capacity):
    flat_routes = routes.reshape(-1)
    entries = flat_routes.shape[0]
    onehot = (flat_routes[:, None] == jnp.arange(experts, dtype=jnp.int32)[None, :]).astype(
        jnp.int32
    )
    before = jnp.cumsum(onehot, 0) - onehot
    position = jnp.sum(before * onehot, 1)
    slot_of = flat_routes * capacity + position
    source = (
        jnp.full((experts * capacity,), entries, jnp.int32)
        .at[slot_of]
        .set(jnp.arange(entries, dtype=jnp.int32))
    )
    return (slot_of, source)


def serve_rows(received, up_half, down_half):
    sources = received.shape[0]
    slots = received.shape[2]
    model_width = received.shape[3]
    row_count = sources * slots
    rows_fwd = received[:, 0].reshape(row_count, model_width)
    rows_saved = received[:, 1].reshape(row_count, model_width)
    rows_grad = received[:, 2].reshape(row_count, model_width)
    against_rows = (((1,), (1,)), ((), ()))
    hidden = jax.nn.silu(jnp.dot(rows_fwd, up_half, preferred_element_type=jnp.float32)).astype(
        jnp.bfloat16
    )
    part_fwd = jnp.dot(hidden, down_half, preferred_element_type=jnp.float32).astype(jnp.bfloat16)
    pre_act = jnp.dot(rows_saved, up_half, preferred_element_type=jnp.float32)
    hidden_grad = lax.dot_general(
        rows_grad, down_half, against_rows, preferred_element_type=jnp.float32
    )
    pre_grad = (hidden_grad * silu_grad(pre_act)).astype(jnp.bfloat16)
    part_bwd = lax.dot_general(
        pre_grad, up_half, against_rows, preferred_element_type=jnp.float32
    ).astype(jnp.bfloat16)
    return jnp.stack(
        [
            part_fwd.reshape(sources, slots, model_width),
            part_bwd.reshape(sources, slots, model_width),
        ],
        1,
    )


def combine(inputs, routed_rows, affinity):
    tokens = inputs.shape[0]
    top_count = affinity.shape[1]
    weights = affinity / jnp.sum(affinity, -1, keepdims=True)
    routed = routed_rows.reshape(tokens, top_count, inputs.shape[1]).astype(jnp.float32)
    return (inputs.astype(jnp.float32) + jnp.sum(weights[..., None] * routed, 1)).astype(
        jnp.bfloat16
    )


def general_path(
    x_fwd,
    routes_fwd,
    affinity_fwd,
    x_bwd,
    grad_bwd,
    routes_bwd,
    affinity_bwd,
    up_weight,
    down_weight,
):
    devices = lax.axis_size("expert")
    experts = devices // 2
    tokens = x_fwd.shape[1]
    model_width = x_fwd.shape[2]
    top_count = routes_fwd.shape[2]
    capacity = 3 * tokens * top_count // devices
    half_slots = capacity // 2
    up_half = up_weight[0]
    down_half = down_weight[0]
    slot_fwd, source_fwd = slot_table(routes_fwd[0], experts, capacity)
    slot_bwd, source_bwd = slot_table(routes_bwd[0], experts, capacity)
    zero_row = jnp.zeros((1, model_width), jnp.bfloat16)
    row_table = jnp.concatenate([x_fwd[0], zero_row, x_bwd[0], zero_row, grad_bwd[0], zero_row], 0)
    stride = tokens + 1
    token_fwd = (source_fwd // top_count).reshape(experts, capacity)
    token_bwd = (source_bwd // top_count).reshape(experts, capacity)
    gather_index = jnp.stack([token_fwd, token_bwd + stride, token_bwd + 2 * stride], 1)
    send_index = (
        gather_index.reshape(experts, 3, 2, half_slots)
        .transpose(0, 2, 1, 3)
        .reshape(devices, 3, half_slots)
    )
    outgoing = row_table[send_index]
    received = lax.all_to_all(outgoing, "expert", split_axis=0, concat_axis=0, tiled=True)
    partner = from_partner_2(received, "expert", 0)
    result = serve_rows(jnp.concatenate([received, partner], 2), up_half, down_half)
    piece_slots = received.shape[2]
    from_partner = from_partner_2(result[:, :, piece_slots:], "expert", 0)
    summed = (
        result[:, :, :piece_slots].astype(jnp.float32) + from_partner.astype(jnp.float32)
    ).astype(jnp.bfloat16)
    returned = lax.all_to_all(summed, "expert", split_axis=0, concat_axis=0, tiled=True)
    flat_back = returned.reshape(-1, model_width)

    def back_index(slot_of, member):
        expert_id = slot_of // capacity
        within = slot_of % capacity
        return (
            (2 * expert_id + within // half_slots) * 2 + member
        ) * half_slots + within % half_slots

    index_fwd = back_index(slot_fwd, 0)
    index_bwd = back_index(slot_bwd, 1)
    layer_out = combine(x_fwd[0], flat_back[index_fwd], affinity_fwd[0])
    input_grad = combine(grad_bwd[0], flat_back[index_bwd], affinity_bwd[0])
    fwd_next = shifted(layer_out[None], "section", 1)
    bwd_next = shifted(input_grad[None], "section", -1)
    return (fwd_next, bwd_next)


def line_kernel(
    sizes,
    routes_fwd,
    affinity_fwd,
    routes_bwd,
    affinity_bwd,
    x_fwd,
    x_bwd,
    grad_bwd,
    up,
    down,
    out_fwd,
    out_bwd,
    blocks,
    ups,
    downs,
    tables,
    total,
    slope,
    hidden_grad,
    hidden,
    pre_grad,
    returned,
    final,
    picked,
    piece,
    local_sem,
    table_send,
    table_recv,
    own_send,
    across_send,
    outer_send,
    block_recv,
    up_send,
    up_recv,
    down_send,
    down_recv,
    back_send,
    back_recv,
    shift_send,
    shift_recv,
):
    sections, experts, tokens, capacity, pieces, cut = sizes
    half_rows = tokens // 2
    streams = (x_fwd, x_bwd, grad_bwd)
    section = lax.axis_index("section")
    device = lax.axis_index("expert")
    place, side = device // 2, device % 2
    last = experts - 1
    is_inner = (place > 0) & (place < last)
    is_end = (place == 0) | (place == last)
    across = jnp.where(place < experts // 2, 1, -1)

    def at_place(where):
        return {"expert": where * 2 + side}

    def remote(src, dst, send, recv, target):
        return pltpu.make_async_remote_copy(
            src_ref=src,
            dst_ref=dst,
            send_sem=send,
            recv_sem=recv,
            device_id=target,
            device_id_type=pl.DeviceIdType.MESH,
        )

    partner = {"expert": place * 2 + 1 - side}
    next_section = {"section": lax.rem(section + 1, sections)}
    previous_section = {"section": lax.rem(section + sections - 1, sections)}
    column = [at_place(lax.rem(place + ahead, experts)) for ahead in range(1, experts)]

    barrier = pltpu.get_barrier_semaphore()
    peers = column + [partner, next_section, previous_section]
    for peer in peers:
        pl.semaphore_signal(
            barrier, inc=1, device_id=peer, device_id_type=pl.DeviceIdType.MESH
        )
    pl.semaphore_wait(barrier, len(peers))

    def rows_of(origin):
        return pl.ds(pl.multiple_of(origin * tokens, tokens), tokens)

    def half_of(origin, half):
        return pl.ds(pl.multiple_of(origin * tokens + half * half_rows, half_rows), half_rows)

    def columns_of(index):
        return pl.ds(pl.multiple_of(index * cut, cut), cut)

    def own_copy(stream, way, half):
        return remote(
            streams[stream].at[pl.ds(half * half_rows, half_rows)],
            blocks.at[stream, half_of(place, half)],
            own_send.at[stream, way, half],
            block_recv.at[stream, place, half],
            at_place(place + 1 - 2 * way),
        )

    def send_own(stream):
        for half in range(2):
            for way, allowed in ((0, place < last), (1, place > 0)):

                @pl.when(allowed)
                def _(way=way, half=half):
                    own_copy(stream, way, half).start()

    def wait_half(stream, origin, half):
        block = blocks.at[stream, half_of(origin, half)]
        remote(
            block, block, own_send.at[stream, 0, half], block_recv.at[stream, origin, half], partner
        ).wait_recv()

    def across_copy(stream, half):
        origin = place - across
        block = blocks.at[stream, half_of(origin, half)]
        return remote(
            block,
            block,
            across_send.at[stream, half],
            block_recv.at[stream, origin, half],
            at_place(place + across),
        )

    def send_across(stream, half):
        @pl.when(is_inner)
        def _():
            wait_half(stream, place - across, half)
            across_copy(stream, half).start()

    def outer_copy(stream, steps):
        origin = place + across * steps
        return remote(
            picked.at[stream, steps - 1],
            blocks.at[stream, pl.ds(pl.multiple_of(origin * tokens, tokens), capacity)],
            outer_send.at[stream, steps - 1],
            block_recv.at[stream, origin, 0],
            at_place(place - across),
        )

    def table_row(member, kind, origin, expert):
        return tables[origin, pl.ds((member * 2 + kind) * experts + expert, 1), :]

    def send_outer(stream, steps):
        @pl.when(is_inner)
        def _():
            origin = place + across * steps
            for half in range(2):
                wait_half(stream, origin, half)
            ranks = table_row(min(stream, 1), 1, origin, place - across)
            slots = lax.broadcasted_iota(jnp.int32, (capacity, tokens), 0).astype(jnp.float32)
            pick = jnp.where(slots == ranks, 1.0, 0.0).astype(jnp.bfloat16)

            @pl.loop(0, pieces)
            def _(index):
                picked[stream, steps - 1, :, columns_of(index)] = jnp.dot(
                    pick,
                    blocks[stream, rows_of(origin), columns_of(index)],
                    preferred_element_type=jnp.float32,
                ).astype(jnp.bfloat16)

            outer_copy(stream, steps).start()

    def wait_at_end(stream):
        @pl.when(is_end)
        def _():
            for half in range(2):
                wait_half(stream, place + across, half)
            for steps in (2, 3):
                origin = place + across * steps
                landed = blocks.at[
                    stream, pl.ds(pl.multiple_of(origin * tokens, tokens), capacity)
                ]
                remote(
                    landed,
                    landed,
                    own_send.at[stream, 0, 0],
                    block_recv.at[stream, origin, 0],
                    partner,
                ).wait_recv()

    def up_copy(index):
        rows = columns_of(index)
        return remote(
            up.at[rows], ups.at[1, rows], up_send.at[index], up_recv.at[index], partner
        )

    def down_copy(index):
        rows = columns_of(index)
        return remote(
            down.at[:, rows],
            downs.at[1, :, rows],
            down_send.at[index],
            down_recv.at[index],
            partner,
        )

    send_own(0)

    @pl.loop(0, pieces)
    def _(index):
        up_copy(index).start()

    @pl.loop(0, pieces)
    def _(index):
        down_copy(index).start()

    local = [
        pltpu.make_async_copy(
            streams[stream], blocks.at[stream, rows_of(place)], local_sem.at[stream]
        )
        for stream in range(3)
    ]
    local.append(pltpu.make_async_copy(up, ups.at[0], local_sem.at[3]))
    local.append(pltpu.make_async_copy(down, downs.at[0], local_sem.at[4]))
    for copy in local:
        copy.start()

    row_id = lax.broadcasted_iota(jnp.int32, (tokens, tokens), 0)
    lane_id = lax.broadcasted_iota(jnp.int32, (tokens, tokens), 1)
    earlier = jnp.where(lane_id < row_id, 1.0, 0.0).astype(jnp.bfloat16)
    for member, (routes, affinity) in enumerate(
        ((routes_fwd, affinity_fwd), (routes_bwd, affinity_bwd))
    ):
        weights = affinity[...] / jnp.sum(affinity[...], -1, keepdims=True)
        share = jnp.zeros((tokens, tokens), jnp.float32)
        named = jnp.zeros((tokens, tokens), jnp.float32)
        for choice in range(routes.shape[1]):
            same = routes[:, choice : choice + 1] == lane_id
            share += jnp.where(same, weights[:, choice : choice + 1], 0.0)
            named += jnp.where(same, 1.0, 0.0)
        rank = jnp.dot(earlier, named.astype(jnp.bfloat16), preferred_element_type=jnp.float32)
        rank = jnp.where(named > 0.5, rank, -1.0)
        base = member * 2 * experts
        tables[place, base : base + experts, :] = share.T[:experts]
        tables[place, base + experts : base + 2 * experts, :] = rank.T[:experts]

    table_copies = [
        remote(
            tables.at[place],
            tables.at[place],
            table_send.at[ahead],
            table_recv.at[place],
            column[ahead],
        )
        for ahead in range(experts - 1)
    ]
    for copy in table_copies:
        copy.start()

    @pl.when(is_end)
    def _():
        for stream in range(3):
            for steps in (2, 3):
                start = pl.multiple_of((place + across * steps) * tokens + capacity, 16)
                blocks[stream, pl.ds(start, tokens - capacity), :] = jnp.zeros(
                    (tokens - capacity, blocks.shape[2]), jnp.bfloat16
                )

    for ahead in range(1, experts):
        origin = lax.rem(place + ahead, experts)
        remote(
            tables.at[origin],
            tables.at[origin],
            table_send.at[0],
            table_recv.at[origin],
            partner,
        ).wait_recv()

    def placing(member, origin):
        slots = row_id.astype(jnp.float32)
        lanes = lane_id.astype(jnp.float32)
        distance = jnp.abs(origin - place)
        packed = is_end & (distance > 1)
        ranks = jnp.where(packed, table_row(member, 1, origin, place), lanes[:1])
        share = table_row(member, 0, origin, place)
        weight = jnp.sum(jnp.where(slots == ranks, share, 0.0), 1, keepdims=True)
        rank = jnp.sum(jnp.where(row_id == lane_id, ranks, 0.0), 1, keepdims=True)
        spread = jnp.where(lanes == rank, 1.0, 0.0).astype(jnp.bfloat16)
        return weight, spread

    def project(stream, half):
        total[...] = jnp.zeros(total.shape, jnp.float32)

        @pl.loop(0, pieces)
        def _(index):
            total[...] += jnp.dot(
                blocks[stream, :, columns_of(index)],
                ups[half, columns_of(index), :],
                preferred_element_type=jnp.float32,
            )

    def make_hidden():
        @pl.loop(0, 2)
        def _(half):
            project(0, half)

            @pl.loop(0, experts)
            def _(origin):
                weight, spread = placing(0, origin)
                act = total[rows_of(origin), :]
                value = (act / (1.0 + jnp.exp(-act)) * weight).astype(jnp.bfloat16)
                hidden[half, rows_of(origin), :] = jnp.dot(
                    spread, value, preferred_element_type=jnp.float32
                ).astype(jnp.bfloat16)

    def make_slope():
        @pl.loop(0, 2)
        def _(half):
            project(1, half)

            @pl.loop(0, experts)
            def _(origin):
                weight, _ = placing(1, origin)
                act = total[rows_of(origin), :]
                sigma = 1.0 / (1.0 + jnp.exp(-act))
                slope[half, rows_of(origin), :] = (
                    sigma * (1.0 + act * (1.0 - sigma))
                ) * weight

    def add_hidden_grad(half, index):
        hidden_grad[half] += lax.dot_general(
            blocks[2, :, columns_of(index)],
            downs[half, :, columns_of(index)],
            AGAINST_ROWS,
            preferred_element_type=jnp.float32,
        )

    def start_hidden_grad():
        hidden_grad[...] = jnp.zeros(hidden_grad.shape, jnp.float32)

        @pl.loop(0, 2 * pieces - 1)
        def _(index):
            half = index // pieces
            add_hidden_grad(half, index - half * pieces)

    def make_pre_grad():
        add_hidden_grad(1, pieces - 1)

        @pl.loop(0, 2 * experts)
        def _(index):
            half = index // experts
            origin = index - half * experts
            _, spread = placing(1, origin)
            rows = rows_of(origin)
            value = (hidden_grad[half, rows, :] * slope[half, rows, :]).astype(jnp.bfloat16)
            pre_grad[half, rows, :] = jnp.dot(
                spread, value, preferred_element_type=jnp.float32
            ).astype(jnp.bfloat16)

    def back_copy(member, target, index):
        way = jnp.where(target > place, 1, -1)
        there = place + way
        slot = jnp.where((way < 0) & (target == there), experts, target)
        return remote(
            returned.at[member, target, index],
            returned.at[member, slot, index],
            back_send.at[member, target, index],
            back_recv.at[member, slot, index],
            at_place(there),
        )

    def wait_back(member, slot, index):
        landed = returned.at[member, slot, index]
        remote(
            landed,
            landed,
            back_send.at[member, 0, index],
            back_recv.at[member, slot, index],
            partner,
        ).wait_recv()

    def shift_copy(member, index):
        return remote(
            final.at[member, index],
            (out_fwd, out_bwd)[member].at[:, columns_of(index)],
            shift_send.at[member, index],
            shift_recv.at[member, index],
            (next_section, previous_section)[member],
        )

    def serve(target, member, index):
        rows = rows_of(target)

        @pl.when(member == 0)
        def _():
            piece[...] = jnp.dot(
                hidden[0, rows, :],
                downs[0, :, columns_of(index)],
                preferred_element_type=jnp.float32,
            ) + jnp.dot(
                hidden[1, rows, :],
                downs[1, :, columns_of(index)],
                preferred_element_type=jnp.float32,
            )

        @pl.when(member == 1)
        def _():
            piece[...] = lax.dot_general(
                pre_grad[0, rows, :],
                ups[0, columns_of(index), :],
                AGAINST_ROWS,
                preferred_element_type=jnp.float32,
            ) + lax.dot_general(
                pre_grad[1, rows, :],
                ups[1, columns_of(index), :],
                AGAINST_ROWS,
                preferred_element_type=jnp.float32,
            )

        @pl.when(target != place)
        def _():
            @pl.when(is_inner)
            def _():
                wait_back(member, target, index)
                returned[member, target, index] = (
                    piece[...] + returned[member, target, index].astype(jnp.float32)
                ).astype(jnp.bfloat16)

            @pl.when(is_end)
            def _():
                returned[member, target, index] = piece[...].astype(jnp.bfloat16)

            back_copy(member, target, index).start()

        @pl.when(target == place)
        def _():
            @pl.when(place > 0)
            def _():
                wait_back(member, target, index)
                piece[...] += returned[member, target, index].astype(jnp.float32)

            @pl.when(place < last)
            def _():
                wait_back(member, experts, index)
                piece[...] += returned[member, experts, index].astype(jnp.float32)

            for each in range(2):

                @pl.when(member == each)
                def _(each=each):
                    final[each, index] = (
                        piece[...]
                        + blocks[2 * each, rows, columns_of(index)].astype(jnp.float32)
                    ).astype(jnp.bfloat16)
                    shift_copy(each, index).start()

    send_across(0, 0)
    send_across(0, 1)
    send_own(1)
    send_outer(0, 1)
    send_across(1, 0)
    send_outer(0, 2)
    send_across(1, 1)
    send_own(2)
    send_outer(1, 1)
    send_across(2, 0)
    send_across(2, 1)
    send_outer(1, 2)
    for copy in local:
        copy.wait()
    wait_at_end(0)

    @pl.loop(0, pieces)
    def _(index):
        up_copy(index).wait_recv()

    make_hidden()

    @pl.loop(0, 2 * pieces + last)
    def _(turn):
        @pl.when(turn < pieces)
        def _():
            down_copy(turn).wait_recv()

        @pl.when(turn == 1)
        def _():
            send_outer(2, 1)

        @pl.when(turn == 3)
        def _():
            send_outer(2, 2)

        @pl.when(turn == pieces)
        def _():
            make_pre_grad()

        @pl.loop(0, experts)
        def _(order):
            target = jnp.where(
                order < last - place,
                last - order,
                jnp.where(order < last, order - (last - place), place),
            )
            late = jnp.where(
                target > place,
                place,
                jnp.where(target < place, last - place, jnp.maximum(place, last - place)),
            )
            step = turn - late

            @pl.when((step >= 0) & (step < 2 * pieces))
            def _():
                member = jnp.where(step >= pieces, 1, 0)
                serve(target, member, step - member * pieces)

        @pl.when(turn == pieces - 3)
        def _():
            wait_at_end(1)
            make_slope()

        @pl.when(turn == pieces - 2)
        def _():
            wait_at_end(2)
            start_hidden_grad()

    for stream in range(3):
        for half in range(2):
            for way, allowed in ((0, place < last), (1, place > 0)):

                @pl.when(allowed)
                def _(stream=stream, way=way, half=half):
                    own_copy(stream, way, half).wait_send()

    @pl.when(is_inner)
    def _():
        for stream in range(3):
            for half in range(2):
                across_copy(stream, half).wait_send()
            for steps in (1, 2):
                outer_copy(stream, steps).wait_send()

    for copy in table_copies:
        copy.wait_send()

    @pl.loop(0, pieces)
    def _(index):
        up_copy(index).wait_send()
        down_copy(index).wait_send()
        for member in range(2):

            @pl.loop(1, experts)
            def _(ahead):
                back_copy(member, lax.rem(place + ahead, experts), index).wait_send()

            shift_copy(member, index).wait()


def line_path(
    x_fwd,
    routes_fwd,
    affinity_fwd,
    x_bwd,
    grad_bwd,
    routes_bwd,
    affinity_bwd,
    up_weight,
    down_weight,
):
    devices = lax.axis_size("expert")
    sections = lax.axis_size("section")
    experts = devices // 2
    tokens, width = x_fwd.shape[1:]
    top_count = routes_fwd.shape[2]
    units = up_weight.shape[2]
    capacity = 3 * tokens * top_count // devices
    cut = piece_width(width)
    pieces = width // cut
    rows = experts * tokens
    bf16, f32 = jnp.bfloat16, jnp.float32
    dma = pltpu.SemaphoreType.DMA
    in_vmem = pl.BlockSpec(memory_space=pltpu.VMEM)
    anywhere = pl.BlockSpec(memory_space=pl.ANY)
    outs = pl.pallas_call(
        functools.partial(line_kernel, (sections, experts, tokens, capacity, pieces, cut)),
        name="expert_line",
        out_shape=[jax.ShapeDtypeStruct((tokens, width), bf16)] * 2,
        in_specs=[in_vmem] * 4 + [anywhere] * 5,
        out_specs=[anywhere] * 2,
        scratch_shapes=[
            pltpu.VMEM((3, rows, width), bf16),
            pltpu.VMEM((2, width, units), bf16),
            pltpu.VMEM((2, units, width), bf16),
            pltpu.VMEM((experts, 4 * experts, tokens), f32),
            pltpu.VMEM((rows, units), f32),
            pltpu.VMEM((2, rows, units), f32),
            pltpu.VMEM((2, rows, units), f32),
            pltpu.VMEM((2, rows, units), bf16),
            pltpu.VMEM((2, rows, units), bf16),
            pltpu.VMEM((2, experts + 1, pieces, tokens, cut), bf16),
            pltpu.VMEM((2, pieces, tokens, cut), bf16),
            pltpu.VMEM((3, 2, capacity, width), bf16),
            pltpu.VMEM((tokens, cut), f32),
            dma((5,)),
            dma((experts - 1,)),
            dma((experts,)),
            dma((3, 2, 2)),
            dma((3, 2)),
            dma((3, 2)),
            dma((3, experts, 2)),
            dma((pieces,)),
            dma((pieces,)),
            dma((pieces,)),
            dma((pieces,)),
            dma((2, experts, pieces)),
            dma((2, experts + 1, pieces)),
            dma((2, pieces)),
            dma((2, pieces)),
        ],
        compiler_params=pltpu.CompilerParams(
            collective_id=0, has_side_effects=True, vmem_limit_bytes=60 << 20
        ),
    )(
        routes_fwd[0],
        affinity_fwd[0],
        routes_bwd[0],
        affinity_bwd[0],
        x_fwd[0],
        x_bwd[0],
        grad_bwd[0],
        up_weight[0],
        down_weight[0],
    )
    return tuple(out[None] for out in outs)


def piece_width(width):
    for cut in (512, 256, 128):
        if width % cut == 0:
            return cut
    return 0


def per_device(*args):
    experts = lax.axis_size("expert") // 2
    tokens, width = args[0].shape[1:]
    if experts == 4 and tokens == 128 and piece_width(width):
        return line_path(*args)
    return general_path(*args)


def solution(mesh):
    in_specs = (
        P("section", "expert", None),
        P("section", "expert", None),
        P("section", "expert", None),
        P("section", "expert", None),
        P("section", "expert", None),
        P("section", "expert", None),
        P("section", "expert", None),
        P("section", None, "expert"),
        P("section", "expert", None),
    )
    out_specs = (P("section", "expert", None), P("section", "expert", None))
    return jax.shard_map(
        per_device, mesh=mesh, in_specs=in_specs, out_specs=out_specs, check_vma=False
    )
```

profile of v0, /device:TPU:9, one launch (start us, length us, event | category | flops | bytes accessed | tf_op | source)
XLA Modules:
  0.0 264.0 jit_solution(13295601792386234392)
XLA Ops:
  0.6 1.4 copy.11
  2.0 1.4 copy.12
  3.5 1.4 copy.13
  4.9 1.4 copy.14
  6.3 253.4 %expert_line.1 = (bf16[128,3584]{1,0:T(8,128)(2,1)}, bf16[128,3584]{1,0:T(8,128)(2,1)}) custom-call(s32[128,2]{1,0:T(8,128)} %bitcast.18, f32[128,2]{1,0:T(8,128)} %bitcast.19, s32[128,2]{1,0:T(8,128)} %bitcast.20, f32[128,2]{1,0:T(8,128)} %bitcast.21, bf16[128,3584]{1,0:T(8,128)(2,1)} %bitcast.13, bf16[128,3584]{1,0:T(8,128)(2,1)} %bitcast.14, ...), custom_call_target="tpu_custom_call" | custom-call | tf_op jit(solution)/shard_map/expert_line/pallas_call | solution.py:722
  259.7 2.2 copy.17
  261.9 2.2 copy.18
where the time goes:
time: 268 us; the launch traced here: 264 us
  Pallas kernels  253 us (94%)
  local copies, waits for them, and re-layouts  9.96 us (4%)
    pallas_call x1, Pallas kernels, line_path(): pl.pallas_call(functools.partial(line_kernel, (sections, experts, tokens,...  253 us
    unnamed x6, local copies, waits for them, and re-layouts  9.96 us

commit v1 on v0

--- a/solution.py
+++ b/solution.py
@@ -173,6 +173,7 @@
     returned,
     final,
     picked,
+    expand,
     piece,
     local_sem,
     table_send,
@@ -225,7 +226,40 @@
         pl.semaphore_signal(
             barrier, inc=1, device_id=peer, device_id_type=pl.DeviceIdType.MESH
         )
+
+    row_id = lax.broadcasted_iota(jnp.int32, (tokens, tokens), 0)
+    lane_id = lax.broadcasted_iota(jnp.int32, (tokens, tokens), 1)
+    later = jnp.where(row_id < lane_id, 1.0, 0.0).astype(jnp.bfloat16)
+    expert_id = row_id[:16]
+    for member, (routes, affinity) in enumerate(
+        ((routes_fwd, affinity_fwd), (routes_bwd, affinity_bwd))
+    ):
+        weights = affinity[...] / jnp.sum(affinity[...], 0, keepdims=True)
+        share = jnp.zeros(expert_id.shape, jnp.float32)
+        named = jnp.zeros(expert_id.shape, jnp.float32)
+        for choice in range(routes.shape[0]):
+            same = routes[choice : choice + 1, :] == expert_id
+            share += jnp.where(same, weights[choice : choice + 1, :], 0.0)
+            named += jnp.where(same, 1.0, 0.0)
+        rank = jnp.dot(named.astype(jnp.bfloat16), later, preferred_element_type=jnp.float32)
+        rank = jnp.where(named > 0.5, rank, -1.0)
+        base = member * 2 * experts
+        tables[place, base : base + experts, :] = share[:experts]
+        tables[place, base + experts : base + 2 * experts, :] = rank[:experts]
+
     pl.semaphore_wait(barrier, len(peers))
+    table_copies = [
+        remote(
+            tables.at[place],
+            tables.at[place],
+            table_send.at[ahead],
+            table_recv.at[place],
+            column[ahead],
+        )
+        for ahead in range(experts - 1)
+    ]
+    for copy in table_copies:
+        copy.start()
 
     def rows_of(origin):
         return pl.ds(pl.multiple_of(origin * tokens, tokens), tokens)
@@ -236,27 +270,23 @@
     def columns_of(index):
         return pl.ds(pl.multiple_of(index * cut, cut), cut)
 
-    def own_copy(stream, way, half):
+    def own_copy(stream, half):
         return remote(
             streams[stream].at[pl.ds(half * half_rows, half_rows)],
             blocks.at[stream, half_of(place, half)],
-            own_send.at[stream, way, half],
+            own_send.at[stream, half],
             block_recv.at[stream, place, half],
-            at_place(place + 1 - 2 * way),
+            at_place(place + across),
         )
 
     def send_own(stream):
         for half in range(2):
-            for way, allowed in ((0, place < last), (1, place > 0)):
-
-                @pl.when(allowed)
-                def _(way=way, half=half):
-                    own_copy(stream, way, half).start()
+            own_copy(stream, half).start()
 
     def wait_half(stream, origin, half):
         block = blocks.at[stream, half_of(origin, half)]
         remote(
-            block, block, own_send.at[stream, 0, half], block_recv.at[stream, origin, half], partner
+            block, block, own_send.at[stream, half], block_recv.at[stream, origin, half], partner
         ).wait_recv()
 
     def across_copy(stream, half):
@@ -279,9 +309,9 @@
     def outer_copy(stream, steps):
         origin = place + across * steps
         return remote(
-            picked.at[stream, steps - 1],
+            picked.at[stream, steps],
             blocks.at[stream, pl.ds(pl.multiple_of(origin * tokens, tokens), capacity)],
-            outer_send.at[stream, steps - 1],
+            outer_send.at[stream, steps],
             block_recv.at[stream, origin, 0],
             at_place(place - across),
         )
@@ -293,15 +323,16 @@
         @pl.when(is_inner)
         def _():
             origin = place + across * steps
-            for half in range(2):
-                wait_half(stream, origin, half)
+            if steps:
+                for half in range(2):
+                    wait_half(stream, origin, half)
             ranks = table_row(min(stream, 1), 1, origin, place - across)
             slots = lax.broadcasted_iota(jnp.int32, (capacity, tokens), 0).astype(jnp.float32)
             pick = jnp.where(slots == ranks, 1.0, 0.0).astype(jnp.bfloat16)
 
             @pl.loop(0, pieces)
             def _(index):
-                picked[stream, steps - 1, :, columns_of(index)] = jnp.dot(
+                picked[stream, steps, :, columns_of(index)] = jnp.dot(
                     pick,
                     blocks[stream, rows_of(origin), columns_of(index)],
                     preferred_element_type=jnp.float32,
@@ -312,9 +343,7 @@
     def wait_at_end(stream):
         @pl.when(is_end)
         def _():
-            for half in range(2):
-                wait_half(stream, place + across, half)
-            for steps in (2, 3):
+            for steps in range(1, experts):
                 origin = place + across * steps
                 landed = blocks.at[
                     stream, pl.ds(pl.multiple_of(origin * tokens, tokens), capacity)
@@ -322,7 +351,7 @@
                 remote(
                     landed,
                     landed,
-                    own_send.at[stream, 0, 0],
+                    own_send.at[stream, 0],
                     block_recv.at[stream, origin, 0],
                     partner,
                 ).wait_recv()
@@ -364,68 +393,46 @@
     for copy in local:
         copy.start()
 
-    row_id = lax.broadcasted_iota(jnp.int32, (tokens, tokens), 0)
-    lane_id = lax.broadcasted_iota(jnp.int32, (tokens, tokens), 1)
-    earlier = jnp.where(lane_id < row_id, 1.0, 0.0).astype(jnp.bfloat16)
-    for member, (routes, affinity) in enumerate(
-        ((routes_fwd, affinity_fwd), (routes_bwd, affinity_bwd))
-    ):
-        weights = affinity[...] / jnp.sum(affinity[...], -1, keepdims=True)
-        share = jnp.zeros((tokens, tokens), jnp.float32)
-        named = jnp.zeros((tokens, tokens), jnp.float32)
-        for choice in range(routes.shape[1]):
-            same = routes[:, choice : choice + 1] == lane_id
-            share += jnp.where(same, weights[:, choice : choice + 1], 0.0)
-            named += jnp.where(same, 1.0, 0.0)
-        rank = jnp.dot(earlier, named.astype(jnp.bfloat16), preferred_element_type=jnp.float32)
-        rank = jnp.where(named > 0.5, rank, -1.0)
-        base = member * 2 * experts
-        tables[place, base : base + experts, :] = share.T[:experts]
-        tables[place, base + experts : base + 2 * experts, :] = rank.T[:experts]
-
-    table_copies = [
-        remote(
-            tables.at[place],
-            tables.at[place],
-            table_send.at[ahead],
-            table_recv.at[place],
-            column[ahead],
-        )
-        for ahead in range(experts - 1)
-    ]
-    for copy in table_copies:
-        copy.start()
-
     @pl.when(is_end)
     def _():
         for stream in range(3):
-            for steps in (2, 3):
+            for steps in range(1, experts):
                 start = pl.multiple_of((place + across * steps) * tokens + capacity, 16)
                 blocks[stream, pl.ds(start, tokens - capacity), :] = jnp.zeros(
                     (tokens - capacity, blocks.shape[2]), jnp.bfloat16
                 )
 
-    for ahead in range(1, experts):
-        origin = lax.rem(place + ahead, experts)
-        remote(
-            tables.at[origin],
-            tables.at[origin],
-            table_send.at[0],
-            table_recv.at[origin],
-            partner,
-        ).wait_recv()
-
-    def placing(member, origin):
+    def wait_tables():
+        for ahead in range(1, experts):
+            origin = lax.rem(place + ahead, experts)
+            remote(
+                tables.at[origin],
+                tables.at[origin],
+                table_send.at[0],
+                table_recv.at[origin],
+                partner,
+            ).wait_recv()
+
+    def make_expand():
+        @pl.when(is_inner)
+        def _():
+            @pl.loop(0, 2 * experts)
+            def _(index):
+                member = index // experts
+                origin = index - member * experts
+                ranks = table_row(member, 1, origin, place - across)
+                rank = jnp.sum(jnp.where(row_id == lane_id, ranks, 0.0), 1, keepdims=True)
+                expand[member, origin] = jnp.where(
+                    lane_id.astype(jnp.float32) == rank, 1.0, 0.0
+                ).astype(jnp.bfloat16)
+
+    def weight_of(member, origin):
+        packed = is_end & (origin != place)
         slots = row_id.astype(jnp.float32)
-        lanes = lane_id.astype(jnp.float32)
-        distance = jnp.abs(origin - place)
-        packed = is_end & (distance > 1)
-        ranks = jnp.where(packed, table_row(member, 1, origin, place), lanes[:1])
+        lanes = lane_id[:1].astype(jnp.float32)
+        ranks = jnp.where(packed, table_row(member, 1, origin, place), lanes)
         share = table_row(member, 0, origin, place)
-        weight = jnp.sum(jnp.where(slots == ranks, share, 0.0), 1, keepdims=True)
-        rank = jnp.sum(jnp.where(row_id == lane_id, ranks, 0.0), 1, keepdims=True)
-        spread = jnp.where(lanes == rank, 1.0, 0.0).astype(jnp.bfloat16)
-        return weight, spread
+        return jnp.sum(jnp.where(slots == ranks, share, 0.0), 1, keepdims=True)
 
     def project(stream, half):
         total[...] = jnp.zeros(total.shape, jnp.float32)
@@ -445,11 +452,9 @@
 
             @pl.loop(0, experts)
             def _(origin):
-                weight, spread = placing(0, origin)
                 act = total[rows_of(origin), :]
-                value = (act / (1.0 + jnp.exp(-act)) * weight).astype(jnp.bfloat16)
-                hidden[half, rows_of(origin), :] = jnp.dot(
-                    spread, value, preferred_element_type=jnp.float32
+                hidden[half, rows_of(origin), :] = (
+                    act / (1.0 + jnp.exp(-act)) * weight_of(0, origin)
                 ).astype(jnp.bfloat16)
 
     def make_slope():
@@ -459,7 +464,7 @@
 
             @pl.loop(0, experts)
             def _(origin):
-                weight, _ = placing(1, origin)
+                weight = weight_of(1, origin)
                 act = total[rows_of(origin), :]
                 sigma = 1.0 / (1.0 + jnp.exp(-act))
                 slope[half, rows_of(origin), :] = (
@@ -489,26 +494,24 @@
         def _(index):
             half = index // experts
             origin = index - half * experts
-            _, spread = placing(1, origin)
             rows = rows_of(origin)
-            value = (hidden_grad[half, rows, :] * slope[half, rows, :]).astype(jnp.bfloat16)
-            pre_grad[half, rows, :] = jnp.dot(
-                spread, value, preferred_element_type=jnp.float32
+            pre_grad[half, rows, :] = (
+                hidden_grad[half, rows, :] * slope[half, rows, :]
             ).astype(jnp.bfloat16)
 
-    def back_copy(member, target, index):
+    def back_copy(member, target, index, count):
         way = jnp.where(target > place, 1, -1)
         there = place + way
         slot = jnp.where((way < 0) & (target == there), experts, target)
         return remote(
-            returned.at[member, target, index],
-            returned.at[member, slot, index],
+            returned.at[member, target, index, pl.ds(0, count)],
+            returned.at[member, slot, index, pl.ds(0, count)],
             back_send.at[member, target, index],
             back_recv.at[member, slot, index],
             at_place(there),
         )
 
-    def wait_back(member, slot, index):
+    def add_back(member, slot, index):
         landed = returned.at[member, slot, index]
         remote(
             landed,
@@ -517,6 +520,22 @@
             back_recv.at[member, slot, index],
             partner,
         ).wait_recv()
+        piece[...] += returned[member, slot, index].astype(jnp.float32)
+
+    def add_packed_back(member, slot, index, origin):
+        landed = returned.at[member, slot, index, pl.ds(0, capacity)]
+        remote(
+            landed,
+            landed,
+            back_send.at[member, 0, index],
+            back_recv.at[member, slot, index],
+            partner,
+        ).wait_recv()
+        piece[...] += jnp.dot(
+            expand[member, origin, :, :capacity],
+            returned[member, slot, index, :capacity],
+            preferred_element_type=jnp.float32,
+        )
 
     def shift_copy(member, index):
         return remote(
@@ -558,30 +577,35 @@
 
         @pl.when(target != place)
         def _():
-            @pl.when(is_inner)
-            def _():
-                wait_back(member, target, index)
-                returned[member, target, index] = (
-                    piece[...] + returned[member, target, index].astype(jnp.float32)
-                ).astype(jnp.bfloat16)
-
             @pl.when(is_end)
             def _():
                 returned[member, target, index] = piece[...].astype(jnp.bfloat16)
-
-            back_copy(member, target, index).start()
+                back_copy(member, target, index, capacity).start()
+
+            @pl.when(is_inner)
+            def _():
+                beyond = (target - place) * across > 0
+
+                @pl.when(beyond)
+                def _():
+                    add_packed_back(member, target, index, target)
+
+                @pl.when(jnp.logical_not(beyond))
+                def _():
+                    add_back(member, target, index)
+
+                returned[member, target, index] = piece[...].astype(jnp.bfloat16)
+                back_copy(member, target, index, tokens).start()
 
         @pl.when(target == place)
         def _():
-            @pl.when(place > 0)
+            @pl.when(is_inner)
             def _():
-                wait_back(member, target, index)
-                piece[...] += returned[member, target, index].astype(jnp.float32)
-
-            @pl.when(place < last)
-            def _():
-                wait_back(member, experts, index)
-                piece[...] += returned[member, experts, index].astype(jnp.float32)
+                add_packed_back(
+                    member, jnp.where(across > 0, place, experts), index, place
+                )
+
+            add_back(member, jnp.where(across > 0, experts, place), index)
 
             for each in range(2):
 
@@ -593,20 +617,28 @@
                     ).astype(jnp.bfloat16)
                     shift_copy(each, index).start()
 
+    local[0].wait()
+    send_outer(0, 0)
     send_across(0, 0)
     send_across(0, 1)
     send_own(1)
+    wait_tables()
     send_outer(0, 1)
+    local[1].wait()
+    send_outer(1, 0)
     send_across(1, 0)
     send_outer(0, 2)
     send_across(1, 1)
     send_own(2)
     send_outer(1, 1)
+    local[2].wait()
+    send_outer(2, 0)
     send_across(2, 0)
     send_across(2, 1)
+    make_expand()
     send_outer(1, 2)
-    for copy in local:
-        copy.wait()
+    local[3].wait()
+    local[4].wait()
     wait_at_end(0)
 
     @pl.loop(0, pieces)
@@ -615,7 +647,7 @@
 
     make_hidden()
 
-    @pl.loop(0, 2 * pieces + last)
+    @pl.loop(0, 2 * pieces + last + 3)
     def _(turn):
         @pl.when(turn < pieces)
         def _():
@@ -643,7 +675,7 @@
             late = jnp.where(
                 target > place,
                 place,
-                jnp.where(target < place, last - place, jnp.maximum(place, last - place)),
+                jnp.where(target < place, last - place, last + 3),
             )
             step = turn - late
 
@@ -652,7 +684,7 @@
                 member = jnp.where(step >= pieces, 1, 0)
                 serve(target, member, step - member * pieces)
 
-        @pl.when(turn == pieces - 3)
+        @pl.when(turn == 2)
         def _():
             wait_at_end(1)
             make_slope()
@@ -664,18 +696,14 @@
 
     for stream in range(3):
         for half in range(2):
-            for way, allowed in ((0, place < last), (1, place > 0)):
-
-                @pl.when(allowed)
-                def _(stream=stream, way=way, half=half):
-                    own_copy(stream, way, half).wait_send()
+            own_copy(stream, half).wait_send()
 
     @pl.when(is_inner)
     def _():
         for stream in range(3):
             for half in range(2):
                 across_copy(stream, half).wait_send()
-            for steps in (1, 2):
+            for steps in range(experts - 1):
                 outer_copy(stream, steps).wait_send()
 
     for copy in table_copies:
@@ -689,7 +717,15 @@
 
             @pl.loop(1, experts)
             def _(ahead):
-                back_copy(member, lax.rem(place + ahead, experts), index).wait_send()
+                target = lax.rem(place + ahead, experts)
+
+                @pl.when(is_end)
+                def _():
+                    back_copy(member, target, index, capacity).wait_send()
+
+                @pl.when(is_inner)
+                def _():
+                    back_copy(member, target, index, tokens).wait_send()
 
             shift_copy(member, index).wait()
 
@@ -737,14 +773,15 @@
             pltpu.VMEM((2, rows, units), bf16),
             pltpu.VMEM((2, experts + 1, pieces, tokens, cut), bf16),
             pltpu.VMEM((2, pieces, tokens, cut), bf16),
-            pltpu.VMEM((3, 2, capacity, width), bf16),
+            pltpu.VMEM((3, experts - 1, capacity, width), bf16),
+            pltpu.VMEM((2, experts, tokens, tokens), bf16),
             pltpu.VMEM((tokens, cut), f32),
             dma((5,)),
             dma((experts - 1,)),
             dma((experts,)),
-            dma((3, 2, 2)),
             dma((3, 2)),
             dma((3, 2)),
+            dma((3, experts - 1)),
             dma((3, experts, 2)),
             dma((pieces,)),
             dma((pieces,)),
@@ -759,10 +796,10 @@
             collective_id=0, has_side_effects=True, vmem_limit_bytes=60 << 20
         ),
     )(
-        routes_fwd[0],
-        affinity_fwd[0],
-        routes_bwd[0],
-        affinity_bwd[0],
+        routes_fwd[0].T,
+        affinity_fwd[0].T,
+        routes_bwd[0].T,
+        affinity_bwd[0].T,
         x_fwd[0],
         x_bwd[0],
         grad_bwd[0],

time: 268 us -> 235 us (0.88); the launches traced: 264 us -> 234 us
  Pallas kernels: 253 us -> 229 us
  local copies, waits for them, and re-layouts: 9.96 us -> 4.32 us
    pallas_call x1, Pallas kernels: 253 us -> 229 us  [line_path(): pl.pallas_call(functools.partial(line_kernel, (sections, experts, tokens,...]
    unnamed x6 -> x2, local copies, waits for them, and re-layouts: 9.96 us -> 4.32 us
where the time goes in v1:
time: 235 us; the launch traced here: 234 us
  Pallas kernels  229 us (97%)
  local copies, waits for them, and re-layouts  4.32 us (2%)
    pallas_call x1, Pallas kernels, line_path(): pl.pallas_call(functools.partial(line_kernel, (sections, experts, tokens,...  229 us

profile of v1, /device:TPU:9, one launch (start us, length us, event | category | flops | bytes accessed | tf_op | source)
XLA Modules:
  0.0 234.5 jit_solution(4540348566145400236)
XLA Ops:
  0.6 229.5 %expert_line.1 = (bf16[128,3584]{1,0:T(8,128)(2,1)}, bf16[128,3584]{1,0:T(8,128)(2,1)}) custom-call(s32[2,128]{1,0:T(2,128)} %bitcast.26, f32[2,128]{1,0:T(2,128)} %bitcast.27, s32[2,128]{1,0:T(2,128)} %bitcast.28, f32[2,128]{1,0:T(2,128)} %bitcast.29, bf16[128,3584]{1,0:T(8,128)(2,1)} %bitcast.21, bf16[128,3584]{1,0:T(8,128)(2,1)} %bitcast.22, ...), custom_call_target="tpu_custom_call" | custom-call | tf_op jit(solution)/shard_map/expert_line/pallas_call | solution.py:758
  230.1 2.2 copy.13
  232.3 2.2 copy.14

commit v2 on v1

--- a/solution.py
+++ b/solution.py
@@ -191,7 +191,8 @@
     shift_send,
     shift_recv,
 ):
-    sections, experts, tokens, capacity, pieces, cut = sizes
+    sections, experts, tokens, capacity, pieces, cut, wide = sizes
+    spans = pieces * cut // wide
     half_rows = tokens // 2
     streams = (x_fwd, x_bwd, grad_bwd)
     section = lax.axis_index("section")
@@ -270,6 +271,9 @@
     def columns_of(index):
         return pl.ds(pl.multiple_of(index * cut, cut), cut)
 
+    def span_of(index):
+        return pl.ds(pl.multiple_of(index * wide, wide), wide)
+
     def own_copy(stream, half):
         return remote(
             streams[stream].at[pl.ds(half * half_rows, half_rows)],
@@ -330,11 +334,11 @@
             slots = lax.broadcasted_iota(jnp.int32, (capacity, tokens), 0).astype(jnp.float32)
             pick = jnp.where(slots == ranks, 1.0, 0.0).astype(jnp.bfloat16)
 
-            @pl.loop(0, pieces)
+            @pl.loop(0, spans)
             def _(index):
-                picked[stream, steps, :, columns_of(index)] = jnp.dot(
+                picked[stream, steps, :, span_of(index)] = jnp.dot(
                     pick,
-                    blocks[stream, rows_of(origin), columns_of(index)],
+                    blocks[stream, rows_of(origin), span_of(index)],
                     preferred_element_type=jnp.float32,
                 ).astype(jnp.bfloat16)
 
@@ -357,7 +361,7 @@
                 ).wait_recv()
 
     def up_copy(index):
-        rows = columns_of(index)
+        rows = span_of(index)
         return remote(
             up.at[rows], ups.at[1, rows], up_send.at[index], up_recv.at[index], partner
         )
@@ -374,7 +378,7 @@
 
     send_own(0)
 
-    @pl.loop(0, pieces)
+    @pl.loop(0, spans)
     def _(index):
         up_copy(index).start()
 
@@ -390,7 +394,7 @@
     ]
     local.append(pltpu.make_async_copy(up, ups.at[0], local_sem.at[3]))
     local.append(pltpu.make_async_copy(down, downs.at[0], local_sem.at[4]))
-    for copy in local:
+    for copy in local[:3]:
         copy.start()
 
     @pl.when(is_end)
@@ -437,11 +441,11 @@
     def project(stream, half):
         total[...] = jnp.zeros(total.shape, jnp.float32)
 
-        @pl.loop(0, pieces)
+        @pl.loop(0, spans)
         def _(index):
             total[...] += jnp.dot(
-                blocks[stream, :, columns_of(index)],
-                ups[half, columns_of(index), :],
+                blocks[stream, :, span_of(index)],
+                ups[half, span_of(index), :],
                 preferred_element_type=jnp.float32,
             )
 
@@ -473,8 +477,8 @@
 
     def add_hidden_grad(half, index):
         hidden_grad[half] += lax.dot_general(
-            blocks[2, :, columns_of(index)],
-            downs[half, :, columns_of(index)],
+            blocks[2, :, span_of(index)],
+            downs[half, :, span_of(index)],
             AGAINST_ROWS,
             preferred_element_type=jnp.float32,
         )
@@ -482,13 +486,13 @@
     def start_hidden_grad():
         hidden_grad[...] = jnp.zeros(hidden_grad.shape, jnp.float32)
 
-        @pl.loop(0, 2 * pieces - 1)
+        @pl.loop(0, 2 * spans - 1)
         def _(index):
-            half = index // pieces
-            add_hidden_grad(half, index - half * pieces)
+            half = index // spans
+            add_hidden_grad(half, index - half * spans)
 
     def make_pre_grad():
-        add_hidden_grad(1, pieces - 1)
+        add_hidden_grad(1, spans - 1)
 
         @pl.loop(0, 2 * experts)
         def _(index):
@@ -622,6 +626,8 @@
     send_across(0, 0)
     send_across(0, 1)
     send_own(1)
+    for copy in local[3:]:
+        copy.start()
     wait_tables()
     send_outer(0, 1)
     local[1].wait()
@@ -641,23 +647,26 @@
     local[4].wait()
     wait_at_end(0)
 
-    @pl.loop(0, pieces)
+    @pl.loop(0, spans)
     def _(index):
         up_copy(index).wait_recv()
 
     make_hidden()
 
-    @pl.loop(0, 2 * pieces + last + 3)
+    forward_lag = jnp.where(is_end, 9, 8)
+    backward_lag = jnp.where(is_end, 9, 4)
+
+    @pl.loop(0, 2 * pieces + 9)
     def _(turn):
         @pl.when(turn < pieces)
         def _():
             down_copy(turn).wait_recv()
 
-        @pl.when(turn == 1)
+        @pl.when(turn == pieces // 7)
         def _():
             send_outer(2, 1)
 
-        @pl.when(turn == 3)
+        @pl.when(turn == 3 * pieces // 7)
         def _():
             send_outer(2, 2)
 
@@ -665,7 +674,7 @@
         def _():
             make_pre_grad()
 
-        @pl.loop(0, experts)
+        @pl.loop(0, experts + 1)
         def _(order):
             target = jnp.where(
                 order < last - place,
@@ -673,23 +682,25 @@
                 jnp.where(order < last, order - (last - place), place),
             )
             late = jnp.where(
-                target > place,
-                place,
-                jnp.where(target < place, last - place, last + 3),
+                order < last,
+                jnp.where(target > place, place, last - place),
+                jnp.where(order == last, forward_lag, backward_lag),
             )
             step = turn - late
-
-            @pl.when((step >= 0) & (step < 2 * pieces))
+            low = jnp.where(order > last, pieces, 0)
+            high = jnp.where(order == last, pieces, 2 * pieces)
+
+            @pl.when((step >= low) & (step < high))
             def _():
                 member = jnp.where(step >= pieces, 1, 0)
                 serve(target, member, step - member * pieces)
 
-        @pl.when(turn == 2)
+        @pl.when(turn == 2 * pieces // 7)
         def _():
             wait_at_end(1)
             make_slope()
 
-        @pl.when(turn == pieces - 2)
+        @pl.when(turn == pieces - 1 - wide // cut)
         def _():
             wait_at_end(2)
             start_hidden_grad()
@@ -709,9 +720,12 @@
     for copy in table_copies:
         copy.wait_send()
 
+    @pl.loop(0, spans)
+    def _(index):
+        up_copy(index).wait_send()
+
     @pl.loop(0, pieces)
     def _(index):
-        up_copy(index).wait_send()
         down_copy(index).wait_send()
         for member in range(2):
 
@@ -748,19 +762,21 @@
     top_count = routes_fwd.shape[2]
     units = up_weight.shape[2]
     capacity = 3 * tokens * top_count // devices
-    cut = piece_width(width)
+    wide = piece_width(width)
+    cut = wide // 2
     pieces = width // cut
+    spans = width // wide
     rows = experts * tokens
     bf16, f32 = jnp.bfloat16, jnp.float32
     dma = pltpu.SemaphoreType.DMA
     in_vmem = pl.BlockSpec(memory_space=pltpu.VMEM)
     anywhere = pl.BlockSpec(memory_space=pl.ANY)
     outs = pl.pallas_call(
-        functools.partial(line_kernel, (sections, experts, tokens, capacity, pieces, cut)),
+        functools.partial(line_kernel, (sections, experts, tokens, capacity, pieces, cut, wide)),
         name="expert_line",
-        out_shape=[jax.ShapeDtypeStruct((tokens, width), bf16)] * 2,
+        out_shape=[pltpu.VMEM((tokens, width), bf16)] * 2,
         in_specs=[in_vmem] * 4 + [anywhere] * 5,
-        out_specs=[anywhere] * 2,
+        out_specs=[in_vmem] * 2,
         scratch_shapes=[
             pltpu.VMEM((3, rows, width), bf16),
             pltpu.VMEM((2, width, units), bf16),
@@ -783,8 +799,8 @@
             dma((3, 2)),
             dma((3, experts - 1)),
             dma((3, experts, 2)),
-            dma((pieces,)),
-            dma((pieces,)),
+            dma((spans,)),
+            dma((spans,)),
             dma((pieces,)),
             dma((pieces,)),
             dma((2, experts, pieces)),
@@ -793,7 +809,7 @@
             dma((2, pieces)),
         ],
         compiler_params=pltpu.CompilerParams(
-            collective_id=0, has_side_effects=True, vmem_limit_bytes=60 << 20
+            collective_id=0, has_side_effects=True, vmem_limit_bytes=56 << 20
         ),
     )(
         routes_fwd[0].T,
@@ -810,9 +826,9 @@
 
 
 def piece_width(width):
-    for cut in (512, 256, 128):
-        if width % cut == 0:
-            return cut
+    for wide in (512, 256):
+        if width % wide == 0:
+            return wide
     return 0
 
 

time: 235 us -> 236 us (level); the launches traced: 234 us -> 233 us
  local copies, waits for them, and re-layouts: 4.32 us -> 1.85 us
    unnamed x2, local copies, waits for them, and re-layouts: 4.32 us -> 1.85 us
where the time goes in v2:
time: 236 us; the launch traced here: 233 us
  Pallas kernels  231 us (98%)
    pallas_call x1, Pallas kernels, line_path(): pl.pallas_call(functools.partial(line_kernel, (sections, experts, tokens,...  231 us

profile of v2, /device:TPU:9, one launch (start us, length us, event | category | flops | bytes accessed | tf_op | source)
XLA Modules:
  0.0 233.0 jit_solution(15371905139108135171)
XLA Ops:
  0.6 230.5 %expert_line.1 = (bf16[128,3584]{1,0:T(8,128)(2,1)S(1)}, bf16[128,3584]{1,0:T(8,128)(2,1)S(1)}) custom-call(s32[2,128]{1,0:T(2,128)} %bitcast.26, f32[2,128]{1,0:T(2,128)} %bitcast.27, s32[2,128]{1,0:T(2,128)} %bitcast.28, f32[2,128]{1,0:T(2,128)} %bitcast.29, bf16[128,3584]{1,0:T(8,128)(2,1)} %bitcast.23, bf16[128,3584]{1,0:T(8,128)(2,1)} %bitcast.24, ...), custom_call_target="tpu_custom_call" | custom-call | tf_op jit(solution)/shard_map/expert_line/pallas_call | solution.py:774
  231.1 0.9 copy.13
  232.1 0.9 copy.14

commit v3 on v2

--- a/solution.py
+++ b/solution.py
@@ -653,54 +653,73 @@
 
     make_hidden()
 
-    forward_lag = jnp.where(is_end, 9, 8)
-    backward_lag = jnp.where(is_end, 9, 4)
-
-    @pl.loop(0, 2 * pieces + 9)
-    def _(turn):
-        @pl.when(turn < pieces)
-        def _():
-            down_copy(turn).wait_recv()
-
-        @pl.when(turn == pieces // 7)
+    reach = jnp.where(is_end, last, last - 1)
+    gate = pieces // 2
+
+    def arrived(tick):
+        steady = jnp.where(tick < pieces, tick - 2, jnp.maximum(pieces - 3, tick - 6))
+        return jnp.clip(jnp.minimum(2 * (tick - gate), steady), 0, pieces)
+
+    def own_arrived(tick):
+        early = arrived(jnp.minimum(tick, pieces - 1) - 2)
+        at_end = jnp.where(tick < (1 + last) * pieces, early, pieces)
+        return jnp.where(is_end, at_end, arrived(tick))
+
+    @pl.loop(0, (2 + last) * pieces)
+    def _(tick):
+        @pl.when(tick < pieces)
+        def _():
+            down_copy(tick).wait_recv()
+
+        @pl.when(tick == pieces // 7)
         def _():
             send_outer(2, 1)
 
-        @pl.when(turn == 3 * pieces // 7)
+        @pl.when(tick == 3 * pieces // 7)
         def _():
             send_outer(2, 2)
 
-        @pl.when(turn == pieces)
+        @pl.when(tick == pieces)
         def _():
             make_pre_grad()
 
-        @pl.loop(0, experts + 1)
-        def _(order):
-            target = jnp.where(
-                order < last - place,
-                last - order,
-                jnp.where(order < last, order - (last - place), place),
-            )
-            late = jnp.where(
-                order < last,
-                jnp.where(target > place, place, last - place),
-                jnp.where(order == last, forward_lag, backward_lag),
-            )
-            step = turn - late
-            low = jnp.where(order > last, pieces, 0)
-            high = jnp.where(order == last, pieces, 2 * pieces)
-
-            @pl.when((step >= low) & (step < high))
+        ready = jnp.where(is_end, tick, tick - 1)
+
+        @pl.when((ready >= 0) & (ready < pieces))
+        def _():
+            @pl.loop(0, reach)
+            def _(nearer):
+                serve(place + across * (reach - nearer), 0, ready)
+
+        later_step = tick - pieces - jnp.where(is_end, 0, 2)
+
+        @pl.when((later_step >= 0) & (later_step < (reach + 1) * pieces))
+        def _():
+            nearer = later_step // pieces
+            serve(place + across * (reach - nearer), 1, later_step - nearer * pieces)
+
+        @pl.when(is_inner)
+        def _():
+            @pl.loop(arrived(tick - 1), arrived(tick))
+            def _(index):
+                serve(place - across, 0, index)
+
+            outer_step = later_step - 3
+
+            @pl.when((outer_step >= 0) & (outer_step < pieces))
             def _():
-                member = jnp.where(step >= pieces, 1, 0)
-                serve(target, member, step - member * pieces)
-
-        @pl.when(turn == 2 * pieces // 7)
+                serve(place - across, 1, outer_step)
+
+        @pl.loop(own_arrived(tick - 1), own_arrived(tick))
+        def _(index):
+            serve(place, 0, index)
+
+        @pl.when(tick == 2 * pieces // 7)
         def _():
             wait_at_end(1)
             make_slope()
 
-        @pl.when(turn == pieces - 1 - wide // cut)
+        @pl.when(tick == pieces - 1 - wide // cut)
         def _():
             wait_at_end(2)
             start_hidden_grad()

time: 236 us -> 223 us (0.945); the launches traced: 233 us -> 223 us
  Pallas kernels: 231 us -> 220 us
    pallas_call x1, Pallas kernels: 231 us -> 220 us  [line_path(): pl.pallas_call(functools.partial(line_kernel, (sections, experts, tokens,...]
where the time goes in v3:
time: 223 us
  Pallas kernels  220 us (99%)
    pallas_call x1, Pallas kernels, line_path(): pl.pallas_call(functools.partial(line_kernel, (sections, experts, tokens,...  220 us

profile of v3, /device:TPU:9, one launch (start us, length us, event | category | flops | bytes accessed | tf_op | source)
XLA Modules:
  0.0 223.0 jit_solution(5718249410805305327)
XLA Ops:
  0.6 220.5 %expert_line.1 = (bf16[128,3584]{1,0:T(8,128)(2,1)S(1)}, bf16[128,3584]{1,0:T(8,128)(2,1)S(1)}) custom-call(s32[2,128]{1,0:T(2,128)} %bitcast.26, f32[2,128]{1,0:T(2,128)} %bitcast.27, s32[2,128]{1,0:T(2,128)} %bitcast.28, f32[2,128]{1,0:T(2,128)} %bitcast.29, bf16[128,3584]{1,0:T(8,128)(2,1)} %bitcast.23, bf16[128,3584]{1,0:T(8,128)(2,1)} %bitcast.24, ...), custom_call_target="tpu_custom_call" | custom-call | tf_op jit(solution)/shard_map/expert_line/pallas_call | solution.py:793
  221.1 0.9 copy.13
  222.1 0.9 copy.14

commit v4 on v3

--- a/solution.py
+++ b/solution.py
@@ -161,6 +161,8 @@
     down,
     out_fwd,
     out_bwd,
+    routes,
+    affinities,
     blocks,
     ups,
     downs,
@@ -228,18 +230,31 @@
             barrier, inc=1, device_id=peer, device_id_type=pl.DeviceIdType.MESH
         )
 
+    small = [
+        pltpu.make_async_copy(source, target, local_sem.at[5 + index])
+        for index, (source, target) in enumerate(
+            (
+                (routes_fwd, routes.at[0]),
+                (affinity_fwd, affinities.at[0]),
+                (routes_bwd, routes.at[1]),
+                (affinity_bwd, affinities.at[1]),
+            )
+        )
+    ]
+    for copy in small:
+        copy.start()
     row_id = lax.broadcasted_iota(jnp.int32, (tokens, tokens), 0)
     lane_id = lax.broadcasted_iota(jnp.int32, (tokens, tokens), 1)
     later = jnp.where(row_id < lane_id, 1.0, 0.0).astype(jnp.bfloat16)
     expert_id = row_id[:16]
-    for member, (routes, affinity) in enumerate(
-        ((routes_fwd, affinity_fwd), (routes_bwd, affinity_bwd))
-    ):
-        weights = affinity[...] / jnp.sum(affinity[...], 0, keepdims=True)
+    for copy in small:
+        copy.wait()
+    for member in range(2):
+        weights = affinities[member] / jnp.sum(affinities[member], 0, keepdims=True)
         share = jnp.zeros(expert_id.shape, jnp.float32)
         named = jnp.zeros(expert_id.shape, jnp.float32)
-        for choice in range(routes.shape[0]):
-            same = routes[choice : choice + 1, :] == expert_id
+        for choice in range(routes.shape[1]):
+            same = routes[member, choice : choice + 1, :] == expert_id
             share += jnp.where(same, weights[choice : choice + 1, :], 0.0)
             named += jnp.where(same, 1.0, 0.0)
         rank = jnp.dot(named.astype(jnp.bfloat16), later, preferred_element_type=jnp.float32)
@@ -363,7 +378,7 @@
     def up_copy(index):
         rows = span_of(index)
         return remote(
-            up.at[rows], ups.at[1, rows], up_send.at[index], up_recv.at[index], partner
+            up.at[rows], ups.at[1, rows], up_send.at[0], up_recv.at[0], partner
         )
 
     def down_copy(index):
@@ -371,11 +386,13 @@
         return remote(
             down.at[:, rows],
             downs.at[1, :, rows],
-            down_send.at[index],
+            down_send.at[0],
             down_recv.at[index],
             partner,
         )
 
+    whole_up = remote(up, ups.at[1], up_send.at[0], up_recv.at[0], partner)
+    whole_down = remote(down, downs.at[1], down_send.at[0], down_recv.at[0], partner)
     send_own(0)
 
     @pl.loop(0, spans)
@@ -510,7 +527,7 @@
         return remote(
             returned.at[member, target, index, pl.ds(0, count)],
             returned.at[member, slot, index, pl.ds(0, count)],
-            back_send.at[member, target, index],
+            back_send.at[member, target],
             back_recv.at[member, slot, index],
             at_place(there),
         )
@@ -520,7 +537,7 @@
         remote(
             landed,
             landed,
-            back_send.at[member, 0, index],
+            back_send.at[member, 0],
             back_recv.at[member, slot, index],
             partner,
         ).wait_recv()
@@ -531,7 +548,7 @@
         remote(
             landed,
             landed,
-            back_send.at[member, 0, index],
+            back_send.at[member, 0],
             back_recv.at[member, slot, index],
             partner,
         ).wait_recv()
@@ -545,8 +562,8 @@
         return remote(
             final.at[member, index],
             (out_fwd, out_bwd)[member].at[:, columns_of(index)],
-            shift_send.at[member, index],
-            shift_recv.at[member, index],
+            shift_send.at[member],
+            shift_recv.at[member],
             (next_section, previous_section)[member],
         )
 
@@ -647,9 +664,7 @@
     local[4].wait()
     wait_at_end(0)
 
-    @pl.loop(0, spans)
-    def _(index):
-        up_copy(index).wait_recv()
+    whole_up.wait_recv()
 
     make_hidden()
 
@@ -739,28 +754,57 @@
     for copy in table_copies:
         copy.wait_send()
 
-    @pl.loop(0, spans)
-    def _(index):
-        up_copy(index).wait_send()
-
-    @pl.loop(0, pieces)
-    def _(index):
-        down_copy(index).wait_send()
+    whole_up.wait_send()
+    whole_down.wait_send()
+
+    @pl.loop(1, experts)
+    def _(ahead):
+        target = lax.rem(place + ahead, experts)
         for member in range(2):
 
-            @pl.loop(1, experts)
-            def _(ahead):
-                target = lax.rem(place + ahead, experts)
-
-                @pl.when(is_end)
-                def _():
-                    back_copy(member, target, index, capacity).wait_send()
-
-                @pl.when(is_inner)
-                def _():
-                    back_copy(member, target, index, tokens).wait_send()
-
-            shift_copy(member, index).wait()
+            @pl.when(is_end)
+            def _(member=member):
+                sent = returned.at[member, target, :, pl.ds(0, capacity)]
+                remote(
+                    sent, sent, back_send.at[member, target], back_recv.at[0, 0, 0], partner
+                ).wait_send()
+
+            @pl.when(is_inner)
+            def _(member=member):
+                sent = returned.at[member, target]
+                remote(
+                    sent, sent, back_send.at[member, target], back_recv.at[0, 0, 0], partner
+                ).wait_send()
+
+    for member, out in enumerate((out_fwd, out_bwd)):
+        remote(
+            final.at[member],
+            final.at[member],
+            shift_send.at[member],
+            shift_recv.at[member],
+            partner,
+        ).wait_send()
+        remote(
+            out, out, shift_send.at[member], shift_recv.at[member], partner
+        ).wait_recv()
+
+
+def store_kernel(fwd, bwd, out_fwd, out_bwd, sems):
+    parts = sems.shape[1]
+    rows = fwd.shape[0] // parts
+    copies = []
+    for member, (source, target) in enumerate(((fwd, out_fwd), (bwd, out_bwd))):
+        for part in range(parts):
+            here = pl.ds(part * rows, rows)
+            copies.append(
+                pltpu.make_async_copy(
+                    source.at[here], target.at[here], sems.at[member, part]
+                )
+            )
+    for copy in copies:
+        copy.start()
+    for copy in copies:
+        copy.wait()
 
 
 def line_path(
@@ -794,9 +838,11 @@
         functools.partial(line_kernel, (sections, experts, tokens, capacity, pieces, cut, wide)),
         name="expert_line",
         out_shape=[pltpu.VMEM((tokens, width), bf16)] * 2,
-        in_specs=[in_vmem] * 4 + [anywhere] * 5,
+        in_specs=[anywhere] * 9,
         out_specs=[in_vmem] * 2,
         scratch_shapes=[
+            pltpu.VMEM((2, top_count, tokens), jnp.int32),
+            pltpu.VMEM((2, top_count, tokens), f32),
             pltpu.VMEM((3, rows, width), bf16),
             pltpu.VMEM((2, width, units), bf16),
             pltpu.VMEM((2, units, width), bf16),
@@ -811,21 +857,21 @@
             pltpu.VMEM((3, experts - 1, capacity, width), bf16),
             pltpu.VMEM((2, experts, tokens, tokens), bf16),
             pltpu.VMEM((tokens, cut), f32),
-            dma((5,)),
+            dma((9,)),
             dma((experts - 1,)),
             dma((experts,)),
             dma((3, 2)),
             dma((3, 2)),
             dma((3, experts - 1)),
             dma((3, experts, 2)),
-            dma((spans,)),
-            dma((spans,)),
+            dma((1,)),
+            dma((1,)),
+            dma((1,)),
             dma((pieces,)),
-            dma((pieces,)),
-            dma((2, experts, pieces)),
+            dma((2, experts)),
             dma((2, experts + 1, pieces)),
-            dma((2, pieces)),
-            dma((2, pieces)),
+            dma((2,)),
+            dma((2,)),
         ],
         compiler_params=pltpu.CompilerParams(
             collective_id=0, has_side_effects=True, vmem_limit_bytes=56 << 20
@@ -841,7 +887,15 @@
         up_weight[0],
         down_weight[0],
     )
-    return tuple(out[None] for out in outs)
+    stored = pl.pallas_call(
+        store_kernel,
+        name="store_outputs",
+        out_shape=[jax.ShapeDtypeStruct((tokens, width), bf16)] * 2,
+        in_specs=[in_vmem] * 2,
+        out_specs=[anywhere] * 2,
+        scratch_shapes=[dma((2, 4))],
+    )(*[pltpu.with_memory_space_constraint(out, pltpu.VMEM) for out in outs])
+    return tuple(out[None] for out in stored)
 
 
 def piece_width(width):

time: 223 us -> 220 us (0.987)
    pallas_call x1, Pallas kernels: 220 us -> 218 us  [line_path(): pl.pallas_call(functools.partial(line_kernel, (sections, experts, tokens,...]
where the time goes in v4:
time: 220 us
  Pallas kernels  219 us (100%)
    pallas_call x1, Pallas kernels, line_path(): pl.pallas_call(functools.partial(line_kernel, (sections, experts, tokens,...  218 us

profile of v4, /device:TPU:9, one launch (start us, length us, event | category | flops | bytes accessed | tf_op | source)
XLA Modules:
  0.0 220.1 jit_solution(3724492313147812864)
XLA Ops:
  0.6 218.2 %expert_line.1 = (bf16[128,3584]{1,0:T(8,128)(2,1)S(1)}, bf16[128,3584]{1,0:T(8,128)(2,1)S(1)}) custom-call(s32[2,128]{1,0:T(2,128)} %bitcast.24, f32[2,128]{1,0:T(2,128)} %bitcast.25, s32[2,128]{1,0:T(2,128)} %bitcast.26, f32[2,128]{1,0:T(2,128)} %bitcast.27, bf16[128,3584]{1,0:T(8,128)(2,1)} %bitcast.21, bf16[128,3584]{1,0:T(8,128)(2,1)} %bitcast.22, ...), custom_call_target="tpu_custom_call" | custom-call | tf_op jit(solution)/shard_map/expert_line/pallas_call | solution.py:837
  218.8 1.3 store_outputs.1

commit v5 on v4

--- a/solution.py
+++ b/solution.py
@@ -178,6 +178,7 @@
     expand,
     piece,
     local_sem,
+    small_sem,
     table_send,
     table_recv,
     own_send,
@@ -196,7 +197,6 @@
     sections, experts, tokens, capacity, pieces, cut, wide = sizes
     spans = pieces * cut // wide
     half_rows = tokens // 2
-    streams = (x_fwd, x_bwd, grad_bwd)
     section = lax.axis_index("section")
     device = lax.axis_index("expert")
     place, side = device // 2, device % 2
@@ -230,8 +230,20 @@
             barrier, inc=1, device_id=peer, device_id_type=pl.DeviceIdType.MESH
         )
 
+    def rows_of(origin):
+        return pl.ds(pl.multiple_of(origin * tokens, tokens), tokens)
+
+    def half_of(origin, half):
+        return pl.ds(pl.multiple_of(origin * tokens + half * half_rows, half_rows), half_rows)
+
+    def columns_of(index):
+        return pl.ds(pl.multiple_of(index * cut, cut), cut)
+
+    def span_of(index):
+        return pl.ds(pl.multiple_of(index * wide, wide), wide)
+
     small = [
-        pltpu.make_async_copy(source, target, local_sem.at[5 + index])
+        pltpu.make_async_copy(source, target, small_sem.at[index])
         for index, (source, target) in enumerate(
             (
                 (routes_fwd, routes.at[0]),
@@ -243,6 +255,22 @@
     ]
     for copy in small:
         copy.start()
+    first_rows, other_rows = pl.ds(0, wide), pl.ds(wide, up.shape[0] - wide)
+    local = [
+        pltpu.make_async_copy(source, target, local_sem.at[index])
+        for index, (source, target) in enumerate(
+            (
+                (x_fwd, blocks.at[0, rows_of(place)]),
+                (up.at[first_rows], ups.at[0, first_rows]),
+                (x_bwd, blocks.at[1, rows_of(place)]),
+                (grad_bwd, blocks.at[2, rows_of(place)]),
+                (up.at[other_rows], ups.at[0, other_rows]),
+                (down, downs.at[0]),
+            )
+        )
+    ]
+    local[0].start()
+    local[1].start()
     row_id = lax.broadcasted_iota(jnp.int32, (tokens, tokens), 0)
     lane_id = lax.broadcasted_iota(jnp.int32, (tokens, tokens), 1)
     later = jnp.where(row_id < lane_id, 1.0, 0.0).astype(jnp.bfloat16)
@@ -277,23 +305,11 @@
     for copy in table_copies:
         copy.start()
 
-    def rows_of(origin):
-        return pl.ds(pl.multiple_of(origin * tokens, tokens), tokens)
-
-    def half_of(origin, half):
-        return pl.ds(pl.multiple_of(origin * tokens + half * half_rows, half_rows), half_rows)
-
-    def columns_of(index):
-        return pl.ds(pl.multiple_of(index * cut, cut), cut)
-
-    def span_of(index):
-        return pl.ds(pl.multiple_of(index * wide, wide), wide)
-
     def own_copy(stream, half):
         return remote(
-            streams[stream].at[pl.ds(half * half_rows, half_rows)],
             blocks.at[stream, half_of(place, half)],
-            own_send.at[stream, half],
+            blocks.at[stream, half_of(place, half)],
+            own_send.at[0],
             block_recv.at[stream, place, half],
             at_place(place + across),
         )
@@ -305,7 +321,7 @@
     def wait_half(stream, origin, half):
         block = blocks.at[stream, half_of(origin, half)]
         remote(
-            block, block, own_send.at[stream, half], block_recv.at[stream, origin, half], partner
+            block, block, own_send.at[0], block_recv.at[stream, origin, half], partner
         ).wait_recv()
 
     def across_copy(stream, half):
@@ -314,7 +330,7 @@
         return remote(
             block,
             block,
-            across_send.at[stream, half],
+            across_send.at[0],
             block_recv.at[stream, origin, half],
             at_place(place + across),
         )
@@ -330,7 +346,7 @@
         return remote(
             picked.at[stream, steps],
             blocks.at[stream, pl.ds(pl.multiple_of(origin * tokens, tokens), capacity)],
-            outer_send.at[stream, steps],
+            outer_send.at[0],
             block_recv.at[stream, origin, 0],
             at_place(place - across),
         )
@@ -370,7 +386,7 @@
                 remote(
                     landed,
                     landed,
-                    own_send.at[stream, 0],
+                    own_send.at[0],
                     block_recv.at[stream, origin, 0],
                     partner,
                 ).wait_recv()
@@ -381,38 +397,47 @@
             up.at[rows], ups.at[1, rows], up_send.at[0], up_recv.at[0], partner
         )
 
-    def down_copy(index):
-        rows = columns_of(index)
+    def split_piece(index, part):
+        if part is None:
+            return cut, pl.ds(0, cut), columns_of(index), index
+        width = cut // 2
+        start = pl.multiple_of(part * width, width)
+        columns = pl.ds(pl.multiple_of(index * cut + part * width, width), width)
+        return width, pl.ds(start, width), columns, index + part
+
+    def down_copy(index, part=None):
+        _, _, columns, order = split_piece(index, part)
         return remote(
-            down.at[:, rows],
-            downs.at[1, :, rows],
+            down.at[:, columns],
+            downs.at[1, :, columns],
             down_send.at[0],
-            down_recv.at[index],
+            down_recv.at[order],
             partner,
         )
 
+    first_up = remote(
+        ups.at[0, first_rows], ups.at[1, first_rows], up_send.at[0], up_recv.at[0], partner
+    )
     whole_up = remote(up, ups.at[1], up_send.at[0], up_recv.at[0], partner)
     whole_down = remote(down, downs.at[1], down_send.at[0], down_recv.at[0], partner)
+    local[0].wait()
     send_own(0)
-
-    @pl.loop(0, spans)
+    local[1].wait()
+    first_up.start()
+
+    @pl.loop(1, spans)
     def _(index):
         up_copy(index).start()
 
-    @pl.loop(0, pieces)
+    @pl.loop(0, pieces - 1)
     def _(index):
         down_copy(index).start()
 
-    local = [
-        pltpu.make_async_copy(
-            streams[stream], blocks.at[stream, rows_of(place)], local_sem.at[stream]
-        )
-        for stream in range(3)
-    ]
-    local.append(pltpu.make_async_copy(up, ups.at[0], local_sem.at[3]))
-    local.append(pltpu.make_async_copy(down, downs.at[0], local_sem.at[4]))
-    for copy in local[:3]:
-        copy.start()
+    for part in range(2):
+        down_copy(pieces - 1, part).start()
+
+    local[2].start()
+    local[3].start()
 
     @pl.when(is_end)
     def _():
@@ -503,7 +528,7 @@
     def start_hidden_grad():
         hidden_grad[...] = jnp.zeros(hidden_grad.shape, jnp.float32)
 
-        @pl.loop(0, 2 * spans - 1)
+        @pl.loop(0, 2 * spans - 2)
         def _(index):
             half = index // spans
             add_hidden_grad(half, index - half * spans)
@@ -520,88 +545,71 @@
                 hidden_grad[half, rows, :] * slope[half, rows, :]
             ).astype(jnp.bfloat16)
 
-    def back_copy(member, target, index, count):
-        way = jnp.where(target > place, 1, -1)
-        there = place + way
-        slot = jnp.where((way < 0) & (target == there), experts, target)
-        return remote(
-            returned.at[member, target, index, pl.ds(0, count)],
-            returned.at[member, slot, index, pl.ds(0, count)],
-            back_send.at[member, target],
-            back_recv.at[member, slot, index],
-            at_place(there),
-        )
-
-    def add_back(member, slot, index):
-        landed = returned.at[member, slot, index]
-        remote(
-            landed,
-            landed,
-            back_send.at[member, 0],
-            back_recv.at[member, slot, index],
-            partner,
-        ).wait_recv()
-        piece[...] += returned[member, slot, index].astype(jnp.float32)
-
-    def add_packed_back(member, slot, index, origin):
-        landed = returned.at[member, slot, index, pl.ds(0, capacity)]
-        remote(
-            landed,
-            landed,
-            back_send.at[member, 0],
-            back_recv.at[member, slot, index],
-            partner,
-        ).wait_recv()
-        piece[...] += jnp.dot(
-            expand[member, origin, :, :capacity],
-            returned[member, slot, index, :capacity],
-            preferred_element_type=jnp.float32,
-        )
-
-    def shift_copy(member, index):
-        return remote(
-            final.at[member, index],
-            (out_fwd, out_bwd)[member].at[:, columns_of(index)],
-            shift_send.at[member],
-            shift_recv.at[member],
-            (next_section, previous_section)[member],
-        )
-
-    def serve(target, member, index):
+    def serve(target, member, index, part=None):
+        width, lanes, columns, order = split_piece(index, part)
         rows = rows_of(target)
-
-        @pl.when(member == 0)
-        def _():
-            piece[...] = jnp.dot(
-                hidden[0, rows, :],
-                downs[0, :, columns_of(index)],
-                preferred_element_type=jnp.float32,
-            ) + jnp.dot(
-                hidden[1, rows, :],
-                downs[1, :, columns_of(index)],
+        sum_ref = piece.at[:, pl.ds(0, width)]
+
+        def back_copy(count):
+            way = jnp.where(target > place, 1, -1)
+            there = place + way
+            slot = jnp.where((way < 0) & (target == there), experts, target)
+            return remote(
+                returned.at[member, target, index, pl.ds(0, count), lanes],
+                returned.at[member, slot, index, pl.ds(0, count), lanes],
+                back_send.at[member, target],
+                back_recv.at[member, slot, order],
+                at_place(there),
+            )
+
+        def wait_back(slot, count):
+            landed = returned.at[member, slot, index, pl.ds(0, count), lanes]
+            remote(
+                landed,
+                landed,
+                back_send.at[member, 0],
+                back_recv.at[member, slot, order],
+                partner,
+            ).wait_recv()
+            return returned[member, slot, index, pl.ds(0, count), lanes]
+
+        def add_back(slot):
+            sum_ref[...] += wait_back(slot, tokens).astype(jnp.float32)
+
+        def add_packed_back(slot):
+            packed = wait_back(slot, capacity)
+            sum_ref[...] += jnp.dot(
+                expand[member, target, :, :capacity],
+                packed,
                 preferred_element_type=jnp.float32,
             )
 
-        @pl.when(member == 1)
-        def _():
-            piece[...] = lax.dot_general(
-                pre_grad[0, rows, :],
-                ups[0, columns_of(index), :],
-                AGAINST_ROWS,
+        def forward_product(half):
+            return jnp.dot(
+                hidden[half, rows, :],
+                downs[half, :, columns],
                 preferred_element_type=jnp.float32,
-            ) + lax.dot_general(
-                pre_grad[1, rows, :],
-                ups[1, columns_of(index), :],
+            )
+
+        def backward_product(half):
+            return lax.dot_general(
+                pre_grad[half, rows, :],
+                ups[half, columns, :],
                 AGAINST_ROWS,
                 preferred_element_type=jnp.float32,
             )
 
+        if member == 0:
+            sum_ref[...] = forward_product(0) + forward_product(1)
+        else:
+            sum_ref[...] = backward_product(0) + backward_product(1)
+
         @pl.when(target != place)
         def _():
             @pl.when(is_end)
             def _():
-                returned[member, target, index] = piece[...].astype(jnp.bfloat16)
-                back_copy(member, target, index, capacity).start()
+                returned[member, target, index, :, lanes] = sum_ref[...].astype(jnp.bfloat16)
+                back_copy(capacity).start()
 
             @pl.when(is_inner)
             def _():
@@ -609,61 +617,71 @@
 
                 @pl.when(beyond)
                 def _():
-                    add_packed_back(member, target, index, target)
+                    add_packed_back(target)
 
                 @pl.when(jnp.logical_not(beyond))
                 def _():
-                    add_back(member, target, index)
-
-                returned[member, target, index] = piece[...].astype(jnp.bfloat16)
-                back_copy(member, target, index, tokens).start()
+                    add_back(target)
+
+                returned[member, target, index, :, lanes] = sum_ref[...].astype(jnp.bfloat16)
+                back_copy(tokens).start()
 
         @pl.when(target == place)
         def _():
             @pl.when(is_inner)
             def _():
-                add_packed_back(
-                    member, jnp.where(across > 0, place, experts), index, place
-                )
-
-            add_back(member, jnp.where(across > 0, experts, place), index)
-
-            for each in range(2):
-
-                @pl.when(member == each)
-                def _(each=each):
-                    final[each, index] = (
-                        piece[...]
-                        + blocks[2 * each, rows, columns_of(index)].astype(jnp.float32)
-                    ).astype(jnp.bfloat16)
-                    shift_copy(each, index).start()
-
-    local[0].wait()
+                add_packed_back(jnp.where(across > 0, place, experts))
+
+            add_back(jnp.where(across > 0, experts, place))
+            final[member, index, :, lanes] = (
+                sum_ref[...] + blocks[2 * member, rows, columns].astype(jnp.float32)
+            ).astype(jnp.bfloat16)
+            remote(
+                final.at[member, index, :, lanes],
+                (out_fwd, out_bwd)[member].at[:, columns],
+                shift_send.at[member],
+                shift_recv.at[member],
+                (next_section, previous_section)[member],
+            ).start()
+
+    def serve_last(target):
+        @pl.loop(0, 2)
+        def _(part):
+            serve(target, 0, pieces - 1, part)
+
+    def serve_forward(target, index):
+        @pl.when(index < pieces - 1)
+        def _():
+            serve(target, 0, index)
+
+        @pl.when(index == pieces - 1)
+        def _():
+            serve_last(target)
+
     send_outer(0, 0)
     send_across(0, 0)
     send_across(0, 1)
+    local[2].wait()
     send_own(1)
-    for copy in local[3:]:
-        copy.start()
+    local[4].start()
+    local[5].start()
     wait_tables()
     send_outer(0, 1)
-    local[1].wait()
     send_outer(1, 0)
     send_across(1, 0)
     send_outer(0, 2)
     send_across(1, 1)
+    local[3].wait()
     send_own(2)
     send_outer(1, 1)
-    local[2].wait()
     send_outer(2, 0)
     send_across(2, 0)
     send_across(2, 1)
     make_expand()
     send_outer(1, 2)
-    local[3].wait()
     local[4].wait()
+    local[5].wait()
     wait_at_end(0)
-
     whole_up.wait_recv()
 
     make_hidden()
@@ -682,7 +700,7 @@
 
     @pl.loop(0, (2 + last) * pieces)
     def _(tick):
-        @pl.when(tick < pieces)
+        @pl.when(tick < pieces - 1)
         def _():
             down_copy(tick).wait_recv()
 
@@ -700,12 +718,26 @@
 
         ready = jnp.where(is_end, tick, tick - 1)
 
-        @pl.when((ready >= 0) & (ready < pieces))
+        @pl.when((ready >= 0) & (ready < pieces - 1))
         def _():
             @pl.loop(0, reach)
             def _(nearer):
                 serve(place + across * (reach - nearer), 0, ready)
 
+        @pl.when((tick == pieces - 1) | (tick == pieces))
+        def _():
+            @pl.loop(0, 2)
+            def _(part):
+                @pl.when(tick == pieces - 1)
+                def _():
+                    down_copy(pieces - 1, part).wait_recv()
+
+                @pl.when(ready == pieces - 1)
+                def _():
+                    @pl.loop(0, reach)
+                    def _(nearer):
+                        serve(place + across * (reach - nearer), 0, pieces - 1, part)
+
         later_step = tick - pieces - jnp.where(is_end, 0, 2)
 
         @pl.when((later_step >= 0) & (later_step < (reach + 1) * pieces))
@@ -717,7 +749,7 @@
         def _():
             @pl.loop(arrived(tick - 1), arrived(tick))
             def _(index):
-                serve(place - across, 0, index)
+                serve_forward(place - across, index)
 
             outer_step = later_step - 3
 
@@ -727,29 +759,31 @@
 
         @pl.loop(own_arrived(tick - 1), own_arrived(tick))
         def _(index):
-            serve(place, 0, index)
+            serve_forward(place, index)
 
         @pl.when(tick == 2 * pieces // 7)
         def _():
             wait_at_end(1)
             make_slope()
 
-        @pl.when(tick == pieces - 1 - wide // cut)
+        @pl.when(tick == pieces - 2 - wide // cut)
         def _():
             wait_at_end(2)
             start_hidden_grad()
 
-    for stream in range(3):
-        for half in range(2):
-            own_copy(stream, half).wait_send()
+        @pl.when(tick == pieces - 1 - wide // cut)
+        def _():
+            add_hidden_grad(1, spans - 2)
+
+    def wait_sent(sent, semaphore):
+        remote(sent, sent, semaphore, back_recv.at[0, 0, 0], partner).wait_send()
+
+    wait_sent(blocks.at[:, rows_of(place)], own_send.at[0])
 
     @pl.when(is_inner)
     def _():
-        for stream in range(3):
-            for half in range(2):
-                across_copy(stream, half).wait_send()
-            for steps in range(experts - 1):
-                outer_copy(stream, steps).wait_send()
+        wait_sent(blocks.at[:, rows_of(place)], across_send.at[0])
+        wait_sent(picked, outer_send.at[0])
 
     for copy in table_copies:
         copy.wait_send()
@@ -765,16 +799,11 @@
             @pl.when(is_end)
             def _(member=member):
                 sent = returned.at[member, target, :, pl.ds(0, capacity)]
-                remote(
-                    sent, sent, back_send.at[member, target], back_recv.at[0, 0, 0], partner
-                ).wait_send()
+                wait_sent(sent, back_send.at[member, target])
 
             @pl.when(is_inner)
             def _(member=member):
-                sent = returned.at[member, target]
-                remote(
-                    sent, sent, back_send.at[member, target], back_recv.at[0, 0, 0], partner
-                ).wait_send()
+                wait_sent(returned.at[member, target], back_send.at[member, target])
 
     for member, out in enumerate((out_fwd, out_bwd)):
         remote(
@@ -857,19 +886,20 @@
             pltpu.VMEM((3, experts - 1, capacity, width), bf16),
             pltpu.VMEM((2, experts, tokens, tokens), bf16),
             pltpu.VMEM((tokens, cut), f32),
-            dma((9,)),
+            dma((6,)),
+            dma((4,)),
             dma((experts - 1,)),
             dma((experts,)),
-            dma((3, 2)),
-            dma((3, 2)),
-            dma((3, experts - 1)),
+            dma((1,)),
+            dma((1,)),
+            dma((1,)),
             dma((3, experts, 2)),
             dma((1,)),
             dma((1,)),
             dma((1,)),
-            dma((pieces,)),
+            dma((pieces + 1,)),
             dma((2, experts)),
-            dma((2, experts + 1, pieces)),
+            dma((2, experts + 1, pieces + 1)),
             dma((2,)),
             dma((2,)),
         ],

time: 220 us -> 219 us (level)
  no operation moved by 1% of the time
where the time goes in v5:
time: 219 us; the launch traced here: 218 us
  Pallas kernels  218 us (100%)
    pallas_call x1, Pallas kernels, line_path(): pl.pallas_call(functools.partial(line_kernel, (sections, experts, tokens,...  216 us

profile of v5, /device:TPU:9, one launch (start us, length us, event | category | flops | bytes accessed | tf_op | source)
XLA Modules:
  0.0 218.4 jit_solution(7847807789904175791)
XLA Ops:
  0.6 216.5 %expert_line.1 = (bf16[128,3584]{1,0:T(8,128)(2,1)S(1)}, bf16[128,3584]{1,0:T(8,128)(2,1)S(1)}) custom-call(s32[2,128]{1,0:T(2,128)} %bitcast.24, f32[2,128]{1,0:T(2,128)} %bitcast.25, s32[2,128]{1,0:T(2,128)} %bitcast.26, f32[2,128]{1,0:T(2,128)} %bitcast.27, bf16[128,3584]{1,0:T(8,128)(2,1)} %bitcast.21, bf16[128,3584]{1,0:T(8,128)(2,1)} %bitcast.22, ...), custom_call_target="tpu_custom_call" | custom-call | tf_op jit(solution)/shard_map/expert_line/pallas_call | solution.py:866
  217.1 1.3 store_outputs.1

commit v6 on v5

--- a/solution.py
+++ b/solution.py
@@ -191,6 +191,7 @@
     down_recv,
     back_send,
     back_recv,
+    forward_recv,
     shift_send,
     shift_recv,
 ):
@@ -204,6 +205,7 @@
     is_inner = (place > 0) & (place < last)
     is_end = (place == 0) | (place == last)
     across = jnp.where(place < experts // 2, 1, -1)
+    reach = jnp.where(is_end, last, last - 1)
 
     def at_place(where):
         return {"expert": where * 2 + side}
@@ -525,10 +527,8 @@
             preferred_element_type=jnp.float32,
         )
 
-    def start_hidden_grad():
-        hidden_grad[...] = jnp.zeros(hidden_grad.shape, jnp.float32)
-
-        @pl.loop(0, 2 * spans - 2)
+    def grow_hidden_grad(low, high):
+        @pl.loop(low, high)
         def _(index):
             half = index // spans
             add_hidden_grad(half, index - half * spans)
@@ -550,6 +550,11 @@
         rows = rows_of(target)
         sum_ref = piece.at[:, pl.ds(0, width)]
 
+        def arrival(slot, group):
+            if member == 0:
+                return forward_recv.at[group, order]
+            return back_recv.at[slot, index]
+
         def back_copy(count):
             way = jnp.where(target > place, 1, -1)
             there = place + way
@@ -558,29 +563,48 @@
                 returned.at[member, target, index, pl.ds(0, count), lanes],
                 returned.at[member, slot, index, pl.ds(0, count), lanes],
                 back_send.at[member, target],
-                back_recv.at[member, slot, order],
+                arrival(slot, jnp.where(is_end, 0, 1)),
                 at_place(there),
             )
 
-        def wait_back(slot, count):
-            landed = returned.at[member, slot, index, pl.ds(0, count), lanes]
-            remote(
-                landed,
-                landed,
-                back_send.at[member, 0],
-                back_recv.at[member, slot, order],
-                partner,
-            ).wait_recv()
-            return returned[member, slot, index, pl.ds(0, count), lanes]
+        def wait_bytes(landed, semaphore):
+            remote(landed, landed, back_send.at[member, 0], semaphore, partner).wait_recv()
+
+        def wait_group(group, count, height):
+            landed = returned.at[0, pl.ds(0, count), index, pl.ds(0, height), lanes]
+            wait_bytes(landed, arrival(None, group))
+
+        def wait_back(slot, height):
+            landed = returned.at[member, slot, index, pl.ds(0, height), lanes]
+            wait_bytes(landed, arrival(slot, None))
 
         def add_back(slot):
-            sum_ref[...] += wait_back(slot, tokens).astype(jnp.float32)
+            if member == 0:
+
+                @pl.when(is_end)
+                def _():
+                    wait_group(1, 1, tokens)
+
+                @pl.when(is_inner & (target != place))
+                def _():
+                    wait_group(1, 2, tokens)
+
+            else:
+                wait_back(slot, tokens)
+            sum_ref[...] += returned[member, slot, index, :, lanes].astype(jnp.float32)
 
         def add_packed_back(slot):
-            packed = wait_back(slot, capacity)
+            if member == 0:
+
+                @pl.when(target == place + across * reach)
+                def _():
+                    wait_group(0, last, capacity)
+
+            else:
+                wait_back(slot, capacity)
             sum_ref[...] += jnp.dot(
                 expand[member, target, :, :capacity],
-                packed,
+                returned[member, slot, index, pl.ds(0, capacity), lanes],
                 preferred_element_type=jnp.float32,
             )
 
@@ -659,22 +683,22 @@
             serve_last(target)
 
     send_outer(0, 0)
+    local[2].wait()
+    send_outer(1, 0)
     send_across(0, 0)
     send_across(0, 1)
-    local[2].wait()
     send_own(1)
     local[4].start()
     local[5].start()
     wait_tables()
     send_outer(0, 1)
-    send_outer(1, 0)
     send_across(1, 0)
     send_outer(0, 2)
     send_across(1, 1)
     local[3].wait()
     send_own(2)
+    send_outer(2, 0)
     send_outer(1, 1)
-    send_outer(2, 0)
     send_across(2, 0)
     send_across(2, 1)
     make_expand()
@@ -686,7 +710,6 @@
 
     make_hidden()
 
-    reach = jnp.where(is_end, last, last - 1)
     gate = pieces // 2
 
     def arrived(tick):
@@ -694,7 +717,7 @@
         return jnp.clip(jnp.minimum(2 * (tick - gate), steady), 0, pieces)
 
     def own_arrived(tick):
-        early = arrived(jnp.minimum(tick, pieces - 1) - 2)
+        early = arrived(jnp.minimum(tick, pieces - 3) - 2)
         at_end = jnp.where(tick < (1 + last) * pieces, early, pieces)
         return jnp.where(is_end, at_end, arrived(tick))
 
@@ -766,17 +789,19 @@
             wait_at_end(1)
             make_slope()
 
-        @pl.when(tick == pieces - 2 - wide // cut)
+        @pl.when(tick == pieces - 5)
         def _():
             wait_at_end(2)
-            start_hidden_grad()
-
-        @pl.when(tick == pieces - 1 - wide // cut)
-        def _():
-            add_hidden_grad(1, spans - 2)
+            hidden_grad[...] = jnp.zeros(hidden_grad.shape, jnp.float32)
+
+        @pl.when((tick >= pieces - 5) & (tick < pieces - 2))
+        def _():
+            third = tick - (pieces - 5)
+            most = 2 * spans - 1
+            grow_hidden_grad(third * most // 3, (third + 1) * most // 3)
 
     def wait_sent(sent, semaphore):
-        remote(sent, sent, semaphore, back_recv.at[0, 0, 0], partner).wait_send()
+        remote(sent, sent, semaphore, back_recv.at[0, 0], partner).wait_send()
 
     wait_sent(blocks.at[:, rows_of(place)], own_send.at[0])
 
@@ -899,7 +924,8 @@
             dma((1,)),
             dma((pieces + 1,)),
             dma((2, experts)),
-            dma((2, experts + 1, pieces + 1)),
+            dma((experts + 1, pieces)),
+            dma((2, pieces + 1)),
             dma((2,)),
             dma((2,)),
         ],
@@ -930,7 +956,7 @@
 
 def piece_width(width):
     for wide in (512, 256):
-        if width % wide == 0:
+        if width % wide == 0 and width >= 4 * wide:
             return wide
     return 0
 

time: 219 us -> 218 us (level)
  no operation moved by 1% of the time
where the time goes in v6:
time: 218 us
  Pallas kernels  217 us (100%)
    pallas_call x1, Pallas kernels, line_path(): pl.pallas_call(functools.partial(line_kernel, (sections, experts, tokens,...  216 us

profile of v6, /device:TPU:9, one launch (start us, length us, event | category | flops | bytes accessed | tf_op | source)
XLA Modules:
  0.0 217.7 jit_solution(15028971872904554345)
XLA Ops:
  0.6 215.8 %expert_line.1 = (bf16[128,3584]{1,0:T(8,128)(2,1)S(1)}, bf16[128,3584]{1,0:T(8,128)(2,1)S(1)}) custom-call(s32[2,128]{1,0:T(2,128)} %bitcast.24, f32[2,128]{1,0:T(2,128)} %bitcast.25, s32[2,128]{1,0:T(2,128)} %bitcast.26, f32[2,128]{1,0:T(2,128)} %bitcast.27, bf16[128,3584]{1,0:T(8,128)(2,1)} %bitcast.21, bf16[128,3584]{1,0:T(8,128)(2,1)} %bitcast.22, ...), custom_call_target="tpu_custom_call" | custom-call | tf_op jit(solution)/shard_map/expert_line/pallas_call | solution.py:891
  216.5 1.3 store_outputs.1

commit v7 on v6

--- a/solution.py
+++ b/solution.py
@@ -223,14 +223,21 @@
     partner = {"expert": place * 2 + 1 - side}
     next_section = {"section": lax.rem(section + 1, sections)}
     previous_section = {"section": lax.rem(section + sections - 1, sections)}
-    column = [at_place(lax.rem(place + ahead, experts)) for ahead in range(1, experts)]
 
     barrier = pltpu.get_barrier_semaphore()
-    peers = column + [partner, next_section, previous_section]
-    for peer in peers:
+
+    def greet(peer):
         pl.semaphore_signal(
             barrier, inc=1, device_id=peer, device_id_type=pl.DeviceIdType.MESH
         )
+
+    for peer in (partner, next_section, previous_section, at_place(place + across)):
+        greet(peer)
+
+    @pl.when(is_inner)
+    def _():
+        greet(at_place(place - across))
+
 
     def rows_of(origin):
         return pl.ds(pl.multiple_of(origin * tokens, tokens), tokens)
@@ -293,19 +300,37 @@
         tables[place, base : base + experts, :] = share[:experts]
         tables[place, base + experts : base + 2 * experts, :] = rank[:experts]
 
-    pl.semaphore_wait(barrier, len(peers))
-    table_copies = [
-        remote(
-            tables.at[place],
-            tables.at[place],
-            table_send.at[ahead],
-            table_recv.at[place],
-            column[ahead],
+    pl.semaphore_wait(barrier, jnp.where(is_end, 4, 5))
+    def table_copy(origin, way, order):
+        return remote(
+            tables.at[origin],
+            tables.at[origin],
+            table_send.at[order],
+            table_recv.at[origin],
+            at_place(place + way),
         )
-        for ahead in range(experts - 1)
-    ]
-    for copy in table_copies:
-        copy.start()
+
+    def wait_table(origin):
+        table_copy(origin, across, 0).wait_recv()
+
+    routes_of_tables = (
+        (place, -across),
+        (place - across, across),
+        (place + across, -across),
+        (place + 2 * across, -across),
+    )
+
+    def pass_table(order):
+        origin, way = routes_of_tables[order]
+        if order:
+            wait_table(origin)
+        table_copy(origin, way, 1 + order).start()
+
+    table_copy(place, across, 0).start()
+
+    @pl.when(is_inner)
+    def _():
+        pass_table(0)
 
     def own_copy(stream, half):
         return remote(
@@ -451,15 +476,14 @@
                 )
 
     def wait_tables():
-        for ahead in range(1, experts):
-            origin = lax.rem(place + ahead, experts)
-            remote(
-                tables.at[origin],
-                tables.at[origin],
-                table_send.at[0],
-                table_recv.at[origin],
-                partner,
-            ).wait_recv()
+        @pl.when(is_inner)
+        def _():
+            pass_table(3)
+
+        @pl.when(is_end)
+        def _():
+            for steps in range(1, experts):
+                wait_table(place + across * steps)
 
     def make_expand():
         @pl.when(is_inner)
@@ -681,6 +705,11 @@
         @pl.when(index == pieces - 1)
         def _():
             serve_last(target)
+
+    @pl.when(is_inner)
+    def _():
+        pass_table(1)
+        pass_table(2)
 
     send_outer(0, 0)
     local[2].wait()
@@ -810,8 +839,12 @@
         wait_sent(blocks.at[:, rows_of(place)], across_send.at[0])
         wait_sent(picked, outer_send.at[0])
 
-    for copy in table_copies:
-        copy.wait_send()
+    table_copy(place, across, 0).wait_send()
+
+    @pl.when(is_inner)
+    def _():
+        for order, (origin, way) in enumerate(routes_of_tables):
+            table_copy(origin, way, 1 + order).wait_send()
 
     whole_up.wait_send()
     whole_down.wait_send()
@@ -913,7 +946,7 @@
             pltpu.VMEM((tokens, cut), f32),
             dma((6,)),
             dma((4,)),
-            dma((experts - 1,)),
+            dma((5,)),
             dma((experts,)),
             dma((1,)),
             dma((1,)),

time: 218 us -> 217 us (level)
  no operation moved by 1% of the time
where the time goes in v7:
time: 217 us; the launch traced here: 216 us
  Pallas kernels  215 us (99%)
    pallas_call x1, Pallas kernels, line_path(): pl.pallas_call(functools.partial(line_kernel, (sections, experts, tokens,...  214 us

profile of v7, /device:TPU:9, one launch (start us, length us, event | category | flops | bytes accessed | tf_op | source)
XLA Modules:
  0.0 215.8 jit_solution(10018006182653731115)
XLA Ops:
  0.6 213.9 %expert_line.1 = (bf16[128,3584]{1,0:T(8,128)(2,1)S(1)}, bf16[128,3584]{1,0:T(8,128)(2,1)S(1)}) custom-call(s32[2,128]{1,0:T(2,128)} %bitcast.24, f32[2,128]{1,0:T(2,128)} %bitcast.25, s32[2,128]{1,0:T(2,128)} %bitcast.26, f32[2,128]{1,0:T(2,128)} %bitcast.27, bf16[128,3584]{1,0:T(8,128)(2,1)} %bitcast.21, bf16[128,3584]{1,0:T(8,128)(2,1)} %bitcast.22, ...), custom_call_target="tpu_custom_call" | custom-call | tf_op jit(solution)/shard_map/expert_line/pallas_call | solution.py:924
  214.5 1.3 store_outputs.1

commit v8 on v7

--- a/solution.py
+++ b/solution.py
@@ -206,6 +206,7 @@
     is_end = (place == 0) | (place == last)
     across = jnp.where(place < experts // 2, 1, -1)
     reach = jnp.where(is_end, last, last - 1)
+    farthest = place + across * reach
 
     def at_place(where):
         return {"expert": where * 2 + side}
@@ -587,7 +588,7 @@
                 returned.at[member, target, index, pl.ds(0, count), lanes],
                 returned.at[member, slot, index, pl.ds(0, count), lanes],
                 back_send.at[member, target],
-                arrival(slot, jnp.where(is_end, 0, 1)),
+                arrival(slot, jnp.where(is_end, jnp.where(target == farthest, 0, 2), 1)),
                 at_place(there),
             )
 
@@ -620,9 +621,13 @@
         def add_packed_back(slot):
             if member == 0:
 
-                @pl.when(target == place + across * reach)
+                @pl.when(target == farthest)
                 def _():
-                    wait_group(0, last, capacity)
+                    wait_group(0, 1, capacity)
+
+                @pl.when(target == place + across)
+                def _():
+                    wait_group(2, last - 1, capacity)
 
             else:
                 wait_back(slot, capacity)
@@ -958,7 +963,7 @@
             dma((pieces + 1,)),
             dma((2, experts)),
             dma((experts + 1, pieces)),
-            dma((2, pieces + 1)),
+            dma((3, pieces + 1)),
             dma((2,)),
             dma((2,)),
         ],
@@ -982,7 +987,7 @@
         out_shape=[jax.ShapeDtypeStruct((tokens, width), bf16)] * 2,
         in_specs=[in_vmem] * 2,
         out_specs=[anywhere] * 2,
-        scratch_shapes=[dma((2, 4))],
+        scratch_shapes=[dma((2, 2))],
     )(*[pltpu.with_memory_space_constraint(out, pltpu.VMEM) for out in outs])
     return tuple(out[None] for out in stored)
 

time: 217 us -> 217 us (level)
  no operation moved by 1% of the time
where the time goes in v8:
time: 217 us; the launch traced here: 216 us
  Pallas kernels  215 us (99%)
    pallas_call x1, Pallas kernels, line_path(): pl.pallas_call(functools.partial(line_kernel, (sections, experts, tokens,...  214 us

profile of v8, /device:TPU:9, one launch (start us, length us, event | category | flops | bytes accessed | tf_op | source)
XLA Modules:
  0.0 215.9 jit_solution(15214936045903073717)
XLA Ops:
  0.6 214.0 %expert_line.1 = (bf16[128,3584]{1,0:T(8,128)(2,1)S(1)}, bf16[128,3584]{1,0:T(8,128)(2,1)S(1)}) custom-call(s32[2,128]{1,0:T(2,128)} %bitcast.24, f32[2,128]{1,0:T(2,128)} %bitcast.25, s32[2,128]{1,0:T(2,128)} %bitcast.26, f32[2,128]{1,0:T(2,128)} %bitcast.27, bf16[128,3584]{1,0:T(8,128)(2,1)} %bitcast.21, bf16[128,3584]{1,0:T(8,128)(2,1)} %bitcast.22, ...), custom_call_target="tpu_custom_call" | custom-call | tf_op jit(solution)/shard_map/expert_line/pallas_call | solution.py:929
  214.7 1.3 store_outputs.1
